TPU v7x, 256 devices: a 4x2x16 block of a 4x16x16 slice. The times are simulated.
256 devices in a mesh: grp: 2 (over y), seq: 128 (over z, x, core).
Axes of the slice: x: 4, y: 2, z: 16, core: 2. Of those that a mesh axis runs over, the one named last changes fastest.
The devices are a block of a 4x16x16 slice.
Arguments:
- frames: bfloat16 [4, 81920, 1280], P('grp', 'seq'), parts along dimension 0, may hold values from -120 to 120
- dec_states: bfloat16 [2, 256, 1280], P(None, 'grp'), parts along dimension 1, may hold values from -6 to 6
- w_query: bfloat16 [1280, 1280], P(None, 'seq'), may hold values from -0.15625 to 0.15625
- w_keyval: bfloat16 [1280, 2560], replicated, may hold values from -0.15625 to 0.15625
- w_output: bfloat16 [1280, 1280], P(None, 'seq'), may hold values from -0.15625 to 0.15625
- head_slope: float32 [20], replicated, may hold values from 0.3 to 12
- lengths: int32 [4, 128], P('grp'), parts along dimension 0, may hold values from 128 to 640, as said below
- positions: int32 [2, 256], P(None, 'grp'), parts along dimension 1, may hold values from 0 to 127
Outputs:
- attended: bfloat16 [2, 256, 1280], P(None, 'grp', 'seq'), parts along dimension 1
There are 2 independent parts, one for each index of `grp`. A program takes and returns all parts, laid end to end along the dimension named above; an argument that names none is the same for every part. Nothing has to cross between parts.
Inputs may be any that keep to these rules, and one draw needn't show every extreme that they name: `lengths`: every step has one block of exactly 640 valid frames.
All inputs are finite; a program needn't handle non-finite values.
Results may differ from a plain program's by a relative error of at most 0.005.
The roundings to bfloat16 on the way count: a program that leaves them out, or rounds other values in their place, can miss the bound.
Values may be sent and summed in bfloat16 or wider, within the bound.
No kernel may reach another device: no remote copies, remote signals or barrier semaphores. Data moves between devices by JAX's collectives and lax.ppermute only.
A program may use at most 128 MiB of HBM per device.

v0:
```python
import functools
import math

import jax
import jax.numpy as jnp
from jax import lax
from jax.sharding import Mesh
from jax.sharding import PartitionSpec as P

SEQ = ("seq_0", "seq_1", "seq_2")


def in_order(tiles, dim):
    tiles = jnp.moveaxis(tiles, 0, dim)
    dims = tiles.shape
    return tiles.reshape(*dims[:dim], dims[dim] * dims[dim + 1], *dims[dim + 2 :])


def all_blocks(x, axes, sequence):
    tiles = x
    for k in sequence:
        tiles = lax.all_gather(tiles, axes[k])
    done = sequence[::-1]
    back = [done.index(k) for k in range(len(axes))]
    tiles = tiles.transpose(*back, *range(len(axes), tiles.ndim))
    return tiles.reshape(-1, *x.shape)


def gathered_by_axis(x, axes, sequence, dim):
    return in_order(all_blocks(x, axes, sequence), dim)


def combined_by_axis(x, axes, combine):
    for axis in axes:
        pieces = jax.tree.map(lambda part: lax.all_gather(part, axis), x)
        x = jax.tree.map(lambda part: part[0], pieces)
        for k in range(1, lax.axis_size(axis)):
            x = combine(x, jax.tree.map(lambda part: part[k], pieces))
    return x


def block_partial(
    queries,
    block_keys,
    block_values,
    length_now,
    slot_place,
    age_steps,
    row_positions,
    head_slope,
    devices,
):
    query_rows, head_count, head_size = queries.shape
    frame_count = block_keys.shape[0]
    keys_split = block_keys.reshape(frame_count, head_count, head_size)
    scores = jnp.einsum(
        "qhd,jhd->hqj", queries, keys_split, preferred_element_type=jnp.float32
    ) / math.sqrt(head_size)
    distance = (
        jnp.abs(row_positions.astype(jnp.float32) - slot_place.astype(jnp.float32)) / devices
        + age_steps
    )
    scores = scores - head_slope[:, None, None] * distance[None, :, None]
    valid = lax.broadcasted_iota(jnp.int32, (1, 1, frame_count), 2) < length_now
    scores = jnp.where(valid, scores, -jnp.inf)
    row_peak = jnp.max(scores, axis=2)
    weights = jnp.exp(scores - row_peak[:, :, None]).astype(jnp.bfloat16)
    row_total = jnp.sum(weights.astype(jnp.float32), axis=2)
    values_split = block_values.reshape(frame_count, head_count, head_size)
    row_context = jnp.einsum(
        "hqj,jhd->qhd", weights, values_split, preferred_element_type=jnp.float32
    )
    return (row_peak.T, row_total.T, row_context.reshape(query_rows, head_count * head_size))


def rescale(row_context, factors, head_count):
    query_rows = row_context.shape[0]
    spread_rows = row_context.reshape(query_rows, head_count, -1) * factors[:, :, None]
    return spread_rows.reshape(query_rows, -1)


def combine_parts(head_count, earlier, later):
    peak_one, total_one, context_one = earlier
    peak_two, total_two, context_two = later
    row_top = jnp.maximum(peak_one, peak_two)
    scale_one = jnp.exp(peak_one - row_top)
    scale_two = jnp.exp(peak_two - row_top)
    merged_total = total_one * scale_one + total_two * scale_two
    merged_context = rescale(context_one, scale_one, head_count) + rescale(
        context_two, scale_two, head_count
    )
    return (row_top, merged_total, merged_context)


def local(frames, dec_states, w_query, w_keyval, w_output, head_slope, lengths, positions):
    devices = lax.axis_size(SEQ)
    own_index = lax.axis_index(SEQ)
    step_count, frame_count, model_width = frames.shape
    query_rows = dec_states.shape[1]
    head_count = head_slope.shape[0]
    head_size = model_width // head_count
    frame_rows = frames.reshape(step_count * frame_count, model_width)
    keyval = jnp.dot(frame_rows, w_keyval, preferred_element_type=jnp.float32).astype(jnp.bfloat16)
    block_keys = keyval[:, :model_width].reshape(step_count, frame_count, model_width)
    block_values = keyval[:, model_width:].reshape(step_count, frame_count, model_width)
    dec_rows = dec_states.reshape(step_count * query_rows, model_width)
    local_query = jnp.dot(dec_rows, w_query, preferred_element_type=jnp.float32).astype(
        jnp.bfloat16
    )
    queries = gathered_by_axis(local_query, SEQ, (0, 1, 2), 1)
    queries = queries.reshape(step_count, query_rows, head_count, head_size)
    combine = functools.partial(combine_parts, head_count)
    slot_place = (own_index + 1) % devices
    results = []
    for step_now in range(step_count):
        running = None
        for older_step in range(step_now + 1):
            partial_now = block_partial(
                queries[step_now],
                block_keys[older_step],
                block_values[older_step],
                lengths[older_step, own_index],
                slot_place,
                float(step_now - older_step),
                positions[step_now],
                head_slope,
                devices,
            )
            running = partial_now if running is None else combine(running, partial_now)
        row_peak, row_total, row_context = running
        row_top, row_total, row_context = combined_by_axis(
            (row_peak, row_total, row_context), SEQ, combine
        )
        context = row_context.reshape(query_rows, head_count, head_size) / row_total[:, :, None]
        context = context.reshape(query_rows, model_width).astype(jnp.bfloat16)
        results.append(
            jnp.dot(context, w_output, preferred_element_type=jnp.float32).astype(jnp.bfloat16)
        )
    return jnp.stack(results)


def solution(mesh):
    finer = Mesh(
        mesh.devices.reshape(mesh.shape["grp"], 16, 4, 2), ("grp", "seq_0", "seq_1", "seq_2")
    )
    return jax.shard_map(
        local,
        mesh=finer,
        in_specs=(
            P("grp", SEQ, None),
            P(None, "grp", None),
            P(None, SEQ),
            P(),
            P(None, SEQ),
            P(),
            P("grp", None),
            P(None, "grp"),
        ),
        out_specs=P(None, "grp", SEQ),
        check_vma=False,
    )
```

profile of v0, /device:TPU:33, one launch (start us, length us, event | category | flops | bytes accessed | tf_op | source)
XLA Modules:
  0.0 570.3 jit_solution(2481648747681104679)
XLA Ops:
  8.5 10.8 %convolution_convert_fusion = bf16[1280,2560]{1,0:T(8,128)(2,1)S(1)} fusion(bf16[1280,1280]{1,0:T(8,128)(2,1)S(1)} %bitcast.1433, bf16[1280,2560]{1,0:T(8,128)(2,1)} %param.11), kind=kOutput, calls=%fused_computation | convolution fusion | flops 8391884800 | bytes 16384000 | tf_op jit(solution)/shard_map/dot_general | solution.py:103
  21.5 3.5 copy.157
  27.6 42.8 %all-gather = bf16[4096,10]{0,1:T(8,128)(2,1)S(1)} all-gather(bf16[256,10]{0,1:T(8,128)(2,1)S(1)} %convolution_convert_fusion.1), channel_id=2, replica_groups=mesh['grp'=2,'seq_0'=16,'seq_1'=4,'seq_2'=2] {'seq_0'}, dimensions={0}, use_global_device_ids=true | all-gather | bytes 87040 | tf_op jit(solution)/shard_map/all_gather | solution.py:22
  70.4 10.2 %all-gather.1 = bf16[64,256,10]{1,0,2:T(8,128)(2,1)S(1)} all-gather(bf16[16,256,10]{1,0,2:T(8,128)(2,1)S(1)} %slice_bitcast_fusion), channel_id=3, replica_groups=mesh['grp'=2,'seq_0'=16,'seq_1'=4,'seq_2'=2] {'seq_1'}, dimensions={0}, use_global_device_ids=true | all-gather | bytes 409600 | tf_op jit(solution)/shard_map/all_gather | solution.py:22
  80.6 12.7 %all-gather.2 = bf16[8,16,256,10]{2,1,0,3:T(8,128)(2,1)S(1)} all-gather(bf16[4,16,256,10]{2,1,0,3:T(8,128)(2,1)S(1)} %bitcast.1442), channel_id=4, replica_groups=mesh['grp'=2,'seq_0'=16,'seq_1'=4,'seq_2'=2] {'seq_2'}, dimensions={0}, use_global_device_ids=true | all-gather | bytes 983040 | tf_op jit(solution)/shard_map/all_gather | solution.py:22
  94.8 2.7 reshape.3589
  102.4 3.5 copy.156
  106.6 2.2 copy.129
  112.2 2.7 fusion.274
  118.6 2.8 fusion
  121.5 4.3 convert_reduce_fusion.2
  131.6 4.1 fusion.259
  136.9 24.8 %all-gather.5 = f32[2048,20]{0,1:T(8,128)S(1)} all-gather(f32[128,20]{0,1:T(8,128)S(1)} %get-tuple-element.190), channel_id=7, replica_groups=mesh['grp'=2,'seq_0'=16,'seq_1'=4,'seq_2'=2] {'seq_0'}, dimensions={0}, use_global_device_ids=true | all-gather | bytes 174080 | tf_op jit(solution)/shard_map/all_gather | solution.py:35
  166.2 84.3 %all-gather.20.cloned.1.call-done = f32[16,128,1280]{2,1,0:T(8,128)} async-done(((f32[1,128,1280]{2,1,0:T(8,128)}), f32[16,128,1280]{2,1,0:T(8,128)}) %all-gather.20.cloned.1.call-update) | async-done | bytes 10485776 | tf_op jit(solution)/shard_map/all_gather | solution.py:35
  250.5 7.2 %fusion.267 = (f32[1,128,1280]{2,1,0:T(8,128)}, f32[1,128,1280]{2,1,0:T(8,128)S(1)}, f32[1,128,1280]{2,1,0:T(8,128)S(1)}, f32[1,128,1280]{2,1,0:T(8,128)S(1)}, f...) fusion(f32[16,128,1280]{2,1,0:T(8,128)} %all-gather.20.cloned.1, ...), kind=kLoop, calls=%fused_computation.595 | loop fusion | bytes 20971520 | tf_op jit(solution)/shard_map/slice | solution.py:36
  264.3 2.2 copy.215
  284.0 5.1 fusion.13
  291.4 27.5 %all-gather.3 = f32[2048,20]{0,1:T(8,128)S(1)} all-gather(f32[128,20]{0,1:T(8,128)S(1)} %bitcast.1449), channel_id=5, replica_groups=mesh['grp'=2,'seq_0'=16,'seq_1'=4,'seq_2'=2] {'seq_0'}, dimensions={0}, use_global_device_ids=true | all-gather | bytes 174080 | tf_op jit(solution)/shard_map/all_gather | solution.py:35
  323.4 53.6 %all-gather.14.cloned.1.call-done = f32[16,128,1280]{2,1,0:T(8,128)} async-done(((f32[1,128,1280]{2,1,0:T(8,128)}), f32[16,128,1280]{2,1,0:T(8,128)}) %all-gather.14.cloned.1.call-update) | async-done | bytes 10485776 | tf_op jit(solution)/shard_map/all_gather | solution.py:35
  377.0 7.1 %fusion.266 = (f32[1,128,1280]{2,1,0:T(8,128)}, f32[1,128,1280]{2,1,0:T(8,128)S(1)}, f32[1,128,1280]{2,1,0:T(8,128)S(1)}, f32[1,128,1280]{2,1,0:T(8,128)S(1)}, f...) fusion(f32[16,128,1280]{2,1,0:T(8,128)} %all-gather.14.cloned.1, ...), kind=kLoop, calls=%fused_computation.594 | loop fusion | bytes 20971520 | tf_op jit(solution)/shard_map/slice | solution.py:36
  392.9 2.2 copy.192
  410.4 5.0 fusion.33
  417.8 22.1 %all-gather.6 = f32[2048,20]{0,1:T(8,128)S(1)} all-gather(f32[128,20]{0,1:T(8,128)} %get-tuple-element.39), channel_id=8, replica_groups=mesh['grp'=2,'seq_0'=16,'seq_1'=4,'seq_2'=2] {'seq_0'}, dimensions={0}, use_global_device_ids=true | all-gather | bytes 174080 | tf_op jit(solution)/shard_map/all_gather | solution.py:35
  440.5 11.0 %all_gather.118 = f32[4,128,20]{1,2,0:T(8,128)S(1)} all-gather(f32[1,128,20]{1,2,0:T(8,128)S(1)} %get-tuple-element.38), channel_id=1, replica_groups=mesh['grp'=2,'seq_0'=16,'seq_1'=4,'seq_2'=2] {'seq_1'}, dimensions={0}, use_global_device_ids=true | all-gather | bytes 51200 | tf_op jit(solution)/shard_map/all_gather | solution.py:35
  458.0 22.3 %all-gather.4 = f32[2048,20]{0,1:T(8,128)S(1)} all-gather(f32[128,20]{0,1:T(8,128)S(1)} %bitcast.1448), channel_id=6, replica_groups=mesh['grp'=2,'seq_0'=16,'seq_1'=4,'seq_2'=2] {'seq_0'}, dimensions={0}, use_global_device_ids=true | all-gather | bytes 174080 | tf_op jit(solution)/shard_map/all_gather | solution.py:35
  480.3 10.7 %all_gather.123 = f32[4,128,20]{1,2,0:T(8,128)} all-gather(f32[1,128,20]{1,2,0:T(8,128)} %get-tuple-element.37), channel_id=1, replica_groups=mesh['grp'=2,'seq_0'=16,'seq_1'=4,'seq_2'=2] {'seq_1'}, dimensions={0}, use_global_device_ids=true | all-gather | bytes 51200 | tf_op jit(solution)/shard_map/all_gather | solution.py:35
  491.1 9.1 %all_gather.107 = f32[4,128,20]{1,2,0:T(8,128)S(1)} all-gather(f32[1,128,20]{1,2,0:T(8,128)S(1)} %get-tuple-element.15), channel_id=1, replica_groups=mesh['grp'=2,'seq_0'=16,'seq_1'=4,'seq_2'=2] {'seq_1'}, dimensions={0}, use_global_device_ids=true | all-gather | bytes 51200 | tf_op jit(solution)/shard_map/all_gather | solution.py:35
  504.5 23.2 %all_gather.124 = f32[2,128,20]{1,2,0:T(8,128)S(1)} all-gather(f32[1,128,20]{1,2,0:T(8,128)S(1)} %get-tuple-element.35), channel_id=1, replica_groups=mesh['grp'=2,'seq_0'=16,'seq_1'=4,'seq_2'=2] {'seq_2'}, dimensions={0}, use_global_device_ids=true | all-gather | bytes 30720 | tf_op jit(solution)/shard_map/all_gather | solution.py:35
  529.6 9.0 %all_gather.112 = f32[4,128,20]{1,2,0:T(8,128)S(1)} all-gather(f32[1,128,20]{1,2,0:T(8,128)S(1)} %get-tuple-element.14), channel_id=1, replica_groups=mesh['grp'=2,'seq_0'=16,'seq_1'=4,'seq_2'=2] {'seq_1'}, dimensions={0}, use_global_device_ids=true | all-gather | bytes 51200 | tf_op jit(solution)/shard_map/all_gather | solution.py:35
  538.7 4.8 all_gather.113
  545.4 2.7 fusion.272
  552.4 2.5 fusion.271
  (154 shorter events, 116.9 us)
Async XLA Ops:
  6.5 1.9 copy-start
  6.6 244.0 %all-gather.20.cloned.1.call-start = ((), (), s32[]{:S(2)}) async-start(), calls=%async_computation.3 | async-start | bytes 11141120 | tf_op jit(solution)/shard_map/all_gather | solution.py:35
  19.3 5.7 %copy-start.13 = (s32[2,128]{1,0:T(2,128)S(1)}, s32[2,128]{1,0:T(2,128)}, u32[]{:S(2)}) copy-start(s32[2,128]{1,0:T(2,128)} %param.14) | copy-start | bytes 3076
  19.3 7.0 %copy-start.12 = (bf16[1280,10]{0,1:T(8,128)(2,1)S(1)}, bf16[1280,10]{0,1:T(8,128)(2,1)}, u32[]{:S(2)}) copy-start(bf16[1280,10]{0,1:T(8,128)(2,1)} %param.10) | copy-start | bytes 76804
  108.8 6.1 %copy-start.14 = (f32[20]{0:T(128)S(1)}, f32[20]{0:T(128)}, u32[]{:S(2)}) copy-start(f32[20]{0:T(128)} %param.13) | copy-start | bytes 244
  112.2 2.8 copy-start.7
  112.2 2.8 copy-start.8
  115.0 3.6 copy-start.3
  115.0 3.6 copy-start.9
  121.5 4.3 copy-start.2
  121.5 4.9 copy-start.6
  131.6 245.4 %all-gather.14.cloned.1.call-start = ((), (), s32[]{:S(2)}) async-start(), calls=%async_computation | async-start | bytes 11141120 | tf_op jit(solution)/shard_map/all_gather | solution.py:35
  136.9 316.0 %all-gather.22.cloned.1.call-start = ((), (), s32[]{:S(2)}) async-start(), calls=%async_computation.4 | async-start | bytes 3276800 | tf_op jit(solution)/shard_map/all_gather | solution.py:35
  291.3 208.9 %all-gather.16.cloned.1.call-start = ((), (), s32[]{:S(2)}) async-start(), calls=%async_computation.1 | async-start | bytes 3276800 | tf_op jit(solution)/shard_map/all_gather | solution.py:35
  318.9 65.2 %copy-start.4 = (f32[2048,20]{0,1:T(8,128)}, f32[2048,20]{0,1:T(8,128)S(1)}, u32[]{:S(2)}) copy-start(f32[2048,20]{0,1:T(8,128)S(1)} %all-gather.3) | copy-start | bytes 491524
  417.7 127.7 %all-gather.24.cloned.1.call-start = ((), (), s32[]{:S(2)}) async-start(), calls=%async_computation.5 | async-start | bytes 1966080 | tf_op jit(solution)/shard_map/all_gather | solution.py:35
  454.8 36.2 %copy-start.5 = (f32[2048,20]{0,1:T(8,128)S(1)}, f32[2048,20]{0,1:T(8,128)}, u32[]{:S(2)}) copy-start(f32[2048,20]{0,1:T(8,128)} %copy-done.4) | copy-start | bytes 491524
  457.9 94.5 %all-gather.18.cloned.1.call-start = ((), (), s32[]{:S(2)}) async-start(), calls=%async_computation.2 | async-start | bytes 1966080 | tf_op jit(solution)/shard_map/all_gather | solution.py:35
  502.2 2.3 copy-start.10
  504.5 56.1 %copy-start.11 = (bf16[1280,10]{0,1:T(8,128)(2,1)S(1)}, bf16[1280,10]{0,1:T(8,128)(2,1)}, u32[]{:S(2)}) copy-start(bf16[1280,10]{0,1:T(8,128)(2,1)} %param.12) | copy-start | bytes 76804
  545.4 17.6 %copy-start.1 = (bf16[2,640,1280]{2,1,0:T(8,128)(2,1)S(1)}, bf16[2,640,1280]{2,1,0:T(8,128)(2,1)}, u32[]{:S(2)}) copy-start(bf16[2,640,1280]{2,1,0:T(8,128)(2,1)} %param.8) | copy-start | bytes 9830404
Sparse Core Ops, SparseCore 0:
  131.7 118.7 all-gather.19
  252.3 124.6 all-gather.13
  378.8 39.2 all-gather.21
  419.8 41.7 all-gather.15
  463.3 21.0 all-gather.23
  504.6 36.4 all-gather.17
where the time goes:
time: 577 us; the launch traced here: 570 us
  blocking collectives  234 us (41%)
  waiting for transfers between devices  138 us (24%)
  local copies, waits for them, and re-layouts  120 us (21%)
  other arithmetic  35.1 us (6%)
  matrix products  27.6 us (5%)
  between operations  14.5 us (3%)
    all_gather x12, blocking collectives, combined_by_axis(): pieces = jax.tree.map(lambda part: lax.all_gather(part, axis), x)  168 us
    all_gather x6, waiting for transfers between devices, combined_by_axis(): pieces = jax.tree.map(lambda part: lax.all_gather(part, axis), x)  138 us
    all_gather x3, blocking collectives, all_blocks(): tiles = lax.all_gather(tiles, axes[k])  65.7 us
    unnamed x75, local copies, waits for them, and re-layouts  63.3 us
    slice x6, local copies, waits for them, and re-layouts, combined_by_axis(): x = jax.tree.map(lambda part: part[0], pieces)  23.3 us
  transfers between devices with their start and end apart: 6, of which 2 were waited for; matrix products, arithmetic and copies ran while one was open for 20% of the time, Pallas kernels for 0%

commit v1 on v0

v1 whole, which is shorter than its diff:
```python
import functools
import math

import jax
import jax.numpy as jnp
from jax import lax
from jax.experimental import pallas as pl
from jax.experimental.pallas import tpu as pltpu
from jax.sharding import Mesh
from jax.sharding import PartitionSpec as P

SEQ = ("seq_0", "seq_1", "seq_2")
BF16 = jnp.bfloat16
F32 = jnp.float32
SLAB = 32
PEAK_ROWS = 3
STAT_ROWS = 5
LOG2E = math.log2(math.e)


def split_rows(x, count):
    rows = []
    for _ in range(count):
        part = x.astype(BF16).astype(F32)
        rows.append(part)
        x = x - part
    return rows


def stat_rows(peak, total):
    return split_rows(peak, PEAK_ROWS) + split_rows(total, STAT_ROWS - PEAK_ROWS)


def attend_kernel(
    lengths_ref, slope_ref, q_ref, k_ref, vt_ref, dist_ref, msg_ref, stat_ref, *, frame_count, chunks
):
    pair = pl.program_id(0)
    head_size = q_ref.shape[0] // 2
    tokens = q_ref.shape[1]
    half = tokens // 2
    scale = 1.0 / math.sqrt(head_size)
    lanes = 2 * head_size

    def keys_of(block):
        keys = k_ref[block * frame_count : (block + 1) * frame_count, :]
        row = lax.broadcasted_iota(jnp.int32, (frame_count, lanes), 0)
        lane = lax.broadcasted_iota(jnp.int32, (frame_count, lanes), 1)
        invalid = jnp.logical_and(row >= lengths_ref[block], lane == 0)
        return jnp.concatenate([keys, jnp.where(invalid, 1.0, 0.0).astype(BF16)], axis=1)

    floor_row = lax.broadcasted_iota(jnp.int32, (lanes, tokens), 0)
    floor = jnp.where(floor_row == 0, -1e30, 0.0).astype(BF16)

    def weigh(keys, right):
        scores = jnp.dot(keys, right, preferred_element_type=F32)
        peak = jnp.max(scores, axis=0, keepdims=True)
        weights = jnp.exp2((scores - peak) * (scale * LOG2E)).astype(BF16)
        return peak * scale, weights

    ones = jnp.ones((16, frame_count), BF16)
    zeros = jnp.zeros((head_size, tokens), BF16)
    zeros_half = jnp.zeros((head_size, half), BF16)
    right = jnp.concatenate(
        [
            jnp.concatenate([q_ref[:head_size, half:], zeros_half], axis=1),
            jnp.concatenate([zeros_half, q_ref[head_size:, half:]], axis=1),
            floor,
        ],
        axis=0,
    )
    new_peak, new_weights = weigh(keys_of(1), right)
    new_sum = jnp.dot(
        jnp.concatenate([vt_ref[:, frame_count:], ones], axis=0),
        new_weights,
        preferred_element_type=F32,
    )
    old_keys = keys_of(0)
    for side in range(2):
        head = 2 * pair + side
        own = q_ref[side * head_size : (side + 1) * head_size, :]
        right = jnp.concatenate([own, zeros, floor] if side == 0 else [zeros, own, floor], axis=0)
        old_peak, old_weights = weigh(old_keys, right)
        old_sum = jnp.dot(
            jnp.concatenate(
                [vt_ref[side * head_size : (side + 1) * head_size, :frame_count], ones], axis=0
            ),
            old_weights,
            preferred_element_type=F32,
        )
        slope = slope_ref[head]
        old_peak = old_peak - slope * dist_ref[0:1, :]
        late_peak = new_peak[:, side * half : (side + 1) * half] - slope * dist_ref[1:2, half:]
        late = slice(side * half, (side + 1) * half)
        top = jnp.maximum(old_peak[:, half:], late_peak)
        old_factor = jnp.exp(old_peak[:, half:] - top)
        new_factor = jnp.exp(late_peak - top)
        old_total = old_sum[head_size : head_size + 1, :]
        new_total = new_sum[2 * head_size : 2 * head_size + 1, late]
        second = (
            old_sum[:head_size, half:] * old_factor
            + new_sum[side * head_size : (side + 1) * head_size, late] * new_factor
        )
        context = jnp.concatenate([old_sum[:head_size, :half], second], axis=1).astype(BF16)
        for part in range(head_size // SLAB):
            slab = head * (head_size // SLAB) + part
            chunk_slabs = (msg_ref.shape[1] - 16) // SLAB
            place = pl.multiple_of((slab % chunk_slabs) * SLAB, SLAB)
            msg_ref[slab // chunk_slabs, pl.ds(place, SLAB), :] = context[
                part * SLAB : (part + 1) * SLAB, :
            ]
        stat_ref[head, 0:1, :] = jnp.concatenate([old_peak[:, :half], top], axis=1)
        stat_ref[head, 1:2, :] = jnp.concatenate(
            [old_total[:, :half], old_total[:, half:] * old_factor + new_total * new_factor], axis=1
        )

    @pl.when(pair == pl.num_programs(0) - 1)
    def _():
        heads = stat_ref.shape[0]
        chunk_rows = msg_ref.shape[1] - 16
        for chunk in range(chunks):
            first = chunk * chunk_rows // head_size
            rows = []
            for head in range(first, first + 3):
                rows += stat_rows(stat_ref[head, 0:1, :], stat_ref[head, 1:2, :])
            rows.append(jnp.zeros_like(rows[0]))
            msg_ref[chunk, chunk_rows:, :] = jnp.concatenate(rows, axis=0).astype(BF16)


def attend(lengths, slope, queries, keys, values_t, dist, frame_count, chunks):
    width, tokens = queries.shape
    head_count = slope.shape[0]
    pair_rows = 2 * (width // head_count)
    rows = keys.shape[0]
    return pl.pallas_call(
        functools.partial(attend_kernel, frame_count=frame_count, chunks=chunks),
        grid=(head_count // 2,),
        in_specs=[
            pl.BlockSpec(memory_space=pltpu.SMEM),
            pl.BlockSpec(memory_space=pltpu.SMEM),
            pl.BlockSpec((pair_rows, tokens), lambda p: (p, 0)),
            pl.BlockSpec((rows, pair_rows), lambda p: (0, p)),
            pl.BlockSpec((pair_rows, rows), lambda p: (p, 0)),
            pl.BlockSpec(dist.shape, lambda p: (0, 0)),
        ],
        out_specs=pl.BlockSpec((chunks, width // chunks + 16, tokens), lambda p: (0, 0, 0)),
        out_shape=jax.ShapeDtypeStruct((chunks, width // chunks + 16, tokens), BF16),
        scratch_shapes=[pltpu.VMEM((head_count, 8, tokens), F32)],
        compiler_params=pltpu.CompilerParams(vmem_limit_bytes=40 << 20),
        name="attend",
    )(lengths, slope, queries, keys, values_t, dist)


def merge_kernel(odd_ref, in_ref, out_ref):
    sources, rows, tokens = in_ref.shape
    chunk_rows = rows - 16
    stats = [in_ref[:, chunk_rows + r, :].astype(F32) for r in range(3 * STAT_ROWS)]
    tops, totals, factors = [], [], []
    for slot in range(3):
        at = slot * STAT_ROWS
        peak = (stats[at] + stats[at + 1]) + stats[at + 2]
        top = jnp.max(peak, axis=0, keepdims=True)
        factor = jnp.exp(peak - top)
        tops.append(top)
        factors.append(factor)
        totals.append(jnp.sum(factor * (stats[at + 3] + stats[at + 4]), axis=0, keepdims=True))
    odd = odd_ref[0] == 1
    slabs, slab_stats = [], []
    for slab in range(chunk_rows // SLAB):
        even_slot, odd_slot = slab // 2, (slab + 1) // 2
        pick = lambda x: x[even_slot] if even_slot == odd_slot else jnp.where(odd, x[odd_slot], x[even_slot])
        factor = pick(factors)
        total = None
        for source in range(sources):
            part = in_ref[source, slab * SLAB : (slab + 1) * SLAB, :].astype(F32)
            part = part * factor[source : source + 1, :]
            total = part if total is None else total + part
        slabs.append(total)
        slab_stats.append(stat_rows(pick(tops), pick(totals)))
    merged = jnp.concatenate(slabs, axis=0)
    targets, out_rows, lanes = out_ref.shape
    pieces = targets // 2
    piece = chunk_rows // pieces
    for target in range(targets):
        side, at = target // pieces, (target % pieces) * piece
        cut = slice(side * lanes, (side + 1) * lanes)
        rows = slab_stats[at // SLAB] + slab_stats[(at + piece - 1) // SLAB]
        rows = [r[:, cut] for r in rows]
        rows.append(jnp.zeros((out_rows - piece - len(rows), lanes), F32))
        out_ref[target] = jnp.concatenate([merged[at : at + piece, cut]] + rows, axis=0).astype(BF16)


def finish_kernel(bound_ref, in_ref, out_ref, *, piece):
    sources, rows, lanes = in_ref.shape
    stats = [in_ref[:, piece + r, :].astype(F32) for r in range(2 * STAT_ROWS)]
    factors, totals = [], []
    for at in (0, STAT_ROWS):
        peak = (stats[at] + stats[at + 1]) + stats[at + 2]
        factor = jnp.exp(peak - jnp.max(peak, axis=0, keepdims=True))
        factors.append(factor)
        totals.append(jnp.sum(factor * (stats[at + 3] + stats[at + 4]), axis=0, keepdims=True))
    out_rows = out_ref.shape[0]
    row = lax.broadcasted_iota(jnp.int32, (out_rows, lanes), 0)
    first = row < bound_ref[0]
    total = None
    for source in range(sources):
        factor = jnp.where(first, factors[0][source : source + 1, :], factors[1][source : source + 1, :])
        part = in_ref[source, :out_rows, :].astype(F32) * factor
        total = part if total is None else total + part
    context = total / jnp.where(first, totals[0], totals[1])
    out_ref[...] = jnp.where(row < piece, context, 0.0).astype(BF16)


def project_kernel(ctx_ref, w_ref, out_ref):
    pieces, sides = ctx_ref.shape[:2]
    for side in range(sides):
        total = None
        for at in range(pieces):
            part = lax.dot_general(
                ctx_ref[at, side], w_ref[at], (((0,), (0,)), ((), ())), preferred_element_type=F32
            )
            total = part if total is None else total + part
        out_ref[side] = total.astype(BF16)


def whole(kernel, out_shape, scalars, arrays, name):
    return pl.pallas_call(
        kernel,
        in_specs=[pl.BlockSpec(memory_space=pltpu.SMEM)] * len(scalars)
        + [pl.BlockSpec(memory_space=pltpu.VMEM)] * len(arrays),
        out_specs=pl.BlockSpec(memory_space=pltpu.VMEM),
        out_shape=out_shape,
        compiler_params=pltpu.CompilerParams(vmem_limit_bytes=32 << 20),
        name=name,
    )(*scalars, *arrays)


def spread(x, axis):
    copies = jnp.broadcast_to(x[None], (lax.axis_size(axis), *x.shape))
    copies = lax.optimization_barrier(copies)
    return lax.all_to_all(copies, axis, 0, 0)


def local(frames, dec_states, w_query, w_keyval, w_output, head_slope, lengths, positions):
    devices = lax.axis_size(SEQ)
    own_index = lax.axis_index(SEQ)
    across, beside, cores = (lax.axis_size(axis) for axis in SEQ)
    step_count, frame_count, width = frames.shape
    query_rows = dec_states.shape[1]
    tokens = step_count * query_rows
    columns = w_query.shape[1]
    near = beside * cores

    own_queries = lax.dot_general(
        w_query,
        dec_states.reshape(tokens, width),
        (((0,), (1,)), ((), ())),
        preferred_element_type=F32,
    ).astype(BF16)
    padded = jnp.pad(own_queries, ((0, 16 - columns), (0, 0)))
    queries = spread(padded, "seq_0")[:, :columns]
    queries = spread(queries.reshape(across * columns, tokens), "seq_1")
    queries = lax.all_gather(queries, "seq_2")
    queries = queries.reshape(cores, beside, across, columns, tokens)
    queries = queries.transpose(2, 1, 0, 3, 4).reshape(width, tokens)

    frame_rows = frames.reshape(step_count * frame_count, width)
    keys = jnp.dot(frame_rows, w_keyval[:, :width], preferred_element_type=F32).astype(BF16)
    values_t = lax.dot_general(
        w_keyval[:, width:], frame_rows, (((0,), (1,)), ((), ())), preferred_element_type=F32
    ).astype(BF16)

    slot_place = ((own_index + 1) % devices).astype(F32)
    apart = jnp.abs(positions.astype(F32) - slot_place) / devices
    age = jnp.arange(step_count, dtype=F32)[:, None]
    dist = jnp.stack([(apart + age).reshape(tokens), apart.reshape(tokens)])
    dist = jnp.pad(dist, ((0, 6), (0, 0)))
    own_lengths = lax.dynamic_slice(lengths, (0, own_index), (step_count, 1)).reshape(step_count)

    message = attend(own_lengths, head_slope, queries, keys, values_t, dist, frame_count, near)
    message = lax.all_to_all(message, ("seq_1", "seq_2"), 0, 0)
    odd = (lax.axis_index(("seq_1", "seq_2")) % 2).astype(jnp.int32).reshape(1)
    piece = 2 * width // devices
    message = whole(
        merge_kernel,
        jax.ShapeDtypeStruct((across, SLAB, tokens // 2), BF16),
        [odd],
        [message],
        "merge",
    )
    message = lax.all_to_all(message, "seq_0", 0, 0)
    at = (lax.axis_index("seq_0") % (across // 2)) * piece
    bound = (SLAB - at % SLAB).astype(jnp.int32).reshape(1)
    context = whole(
        functools.partial(finish_kernel, piece=piece),
        jax.ShapeDtypeStruct((24, tokens // 2), BF16),
        [bound],
        [message],
        "finish",
    )
    context = spread(context, "seq_0")
    context = spread(context.reshape(across * 24, tokens // 2), "seq_1")
    context = lax.all_gather(context, "seq_2")
    context = context.reshape(near, 2, across // 2 * 24, tokens // 2)
    weights = w_output.reshape(beside, cores, across // 2, piece, columns)
    weights = jnp.pad(weights, ((0, 0), (0, 0), (0, 0), (0, 24 - piece), (0, 0)))
    weights = weights.transpose(1, 0, 2, 3, 4).reshape(near, across // 2 * 24, columns)
    return whole(
        project_kernel,
        jax.ShapeDtypeStruct((step_count, query_rows, columns), BF16),
        [],
        [context, weights],
        "project",
    )


def solution(mesh):
    finer = Mesh(
        mesh.devices.reshape(mesh.shape["grp"], 16, 4, 2), ("grp", "seq_0", "seq_1", "seq_2")
    )
    return jax.shard_map(
        local,
        mesh=finer,
        in_specs=(
            P("grp", SEQ, None),
            P(None, "grp", None),
            P(None, SEQ),
            P(),
            P(None, SEQ),
            P(),
            P("grp", None),
            P(None, "grp"),
        ),
        out_specs=P(None, "grp", SEQ),
        check_vma=False,
    )
```

time: 577 us -> 168 us (0.29); the launches traced: 570 us -> 167 us
  blocking collectives: 234 us -> 28.3 us
  waiting for transfers between devices: 138 us -> 32.2 us
  local copies, waits for them, and re-layouts: 120 us -> 21.5 us
  starting transfers between devices: 0.33 us -> 49.3 us
  other arithmetic: 35.1 us -> 0.02 us
  Pallas kernels: 0 us -> 18.7 us
  between operations: 14.5 us -> 0.15 us
  matrix products: 27.6 us -> 17.3 us
    all_gather x15 -> x2, blocking collectives: 234 us -> 11 us  [the longest x1 6.54 us: local(): context = lax.all_gather(context, 'seq_2')]
    all_gather x6 -> x0, waiting for transfers between devices: 138 us -> none  [combined_by_axis(): pieces = jax.tree.map(lambda part: lax.all_gather(part, axis), x)]
    unnamed x75 -> x20, local copies, waits for them, and re-layouts: 63.3 us -> 6.84 us
    all_to_all x0 -> x5, starting transfers between devices: none -> 49.3 us  [the longest x3 33 us: spread(): return lax.all_to_all(copies, axis, 0, 0)]
    slice x14 -> x0, local copies, waits for them, and re-layouts: 40.2 us -> none  [the longest x6 23.3 us: combined_by_axis(): x = jax.tree.map(lambda part: part[0], pieces)]
    all_to_all x0 -> x5, waiting for transfers between devices: none -> 32.2 us  [the longest x1 11.7 us: local(): message = lax.all_to_all(message, 'seq_0', 0, 0)]
    pallas_call x0 -> x4, Pallas kernels: none -> 18.7 us  [the longest x1 16 us: attend(): pl.pallas_call(functools.partial(attend_kernel, frame_count=frame_count,...]
    all_to_all x0 -> x1, blocking collectives: none -> 17.3 us  [spread(): return lax.all_to_all(copies, axis, 0, 0)]
  transfers between devices with their start and end apart: 6 -> 5, of which waited for: 2 -> 4; matrix products, arithmetic and copies ran while one was open for 20% -> 12% of each run, Pallas kernels for 0% -> 0%
where the time goes in v1:
time: 168 us; the launch traced here: 167 us
  starting transfers between devices  49.3 us (29%)
  waiting for transfers between devices  32.2 us (19%)
  blocking collectives  28.3 us (17%)
  local copies, waits for them, and re-layouts  21.5 us (13%)
  Pallas kernels  18.7 us (11%)
  matrix products  17.3 us (10%)
    all_to_all x3, starting transfers between devices, spread(): return lax.all_to_all(copies, axis, 0, 0)  33 us
    all_to_all x1, blocking collectives, spread(): return lax.all_to_all(copies, axis, 0, 0)  17.3 us
    pallas_call x1, Pallas kernels, attend(): pl.pallas_call(functools.partial(attend_kernel, frame_count=frame_count,...  16 us
    all_to_all x1, waiting for transfers between devices, local(): message = lax.all_to_all(message, 'seq_0', 0, 0)  11.7 us
    all_to_all x1, waiting for transfers between devices, local(): message = lax.all_to_all(message, ('seq_1', 'seq_2'), 0, 0)  11.7 us
    all_to_all x1, starting transfers between devices, local(): message = lax.all_to_all(message, 'seq_0', 0, 0)  11.6 us
    all_to_all x3, waiting for transfers between devices, spread(): return lax.all_to_all(copies, axis, 0, 0)  8.79 us
    dot_general x1, matrix products, local(): lax.dot_general(w_keyval[:, width:], frame_rows, (((0,), (1,)), ((), ()))...  8.15 us
  transfers between devices with their start and end apart: 5, of which 4 were waited for; matrix products, arithmetic and copies ran while one was open for 12% of the time, Pallas kernels for 0%

profile of v1, /device:TPU:33, one launch (start us, length us, event | category | flops | bytes accessed | tf_op | source)
XLA Modules:
  0.0 167.4 jit_solution(9700103361470409728)
XLA Ops:
  0.0 1.5 convolution_convert_fusion.2
  1.6 0.7 broadcast_in_dim.12
  2.3 24.5 %all-to-all-start = ((bf16[16,16,256]{2,1,0:T(8,128)(2,1)}), bf16[16,16,256]{2,1,0:T(8,128)(2,1)S(1)}, u32[]{:S(2)}, u32[]{:S(2)}) async-start(bf16[16,16,256]{2,1,0:T(8,128)(2,1)} %broadcast_in_dim.12), calls=%async_computation | async-start | bytes 262144 | tf_op jit(solution)/shard_map/all_to_all | solution.py:240
  26.8 7.7 %convolution_convert_fusion.1.k_ref = bf16[1280,1280]{1,0:T(8,128)(2,1)} fusion(bf16[1280,1280]{1,0:T(8,128)(2,1)S(1)} %bitcast.21, bf16[1280,2560]{1,0:T(8,128)(2,1)} %param.11), kind=kOutput, calls=%fused_computation.1 | convolution fusion | flops 4195942400 | bytes 9830400 | tf_op jit(solution)/shard_map/dot_general | solution.py:267
  34.5 8.2 %convolution_convert_fusion.vt_ref = bf16[1280,1280]{1,0:T(8,128)(2,1)} fusion(bf16[1280,1280]{1,0:T(8,128)(2,1)S(1)} %bitcast.22, bf16[1280,2560]{1,0:T(8,128)(2,1)} %param.11), kind=kOutput, calls=%fused_computation | convolution fusion | flops 4195942400 | bytes 9830400 | tf_op jit(solution)/shard_map/dot_general | solution.py:268
  42.9 0.8 broadcast_in_dim.14
  43.6 4.3 %all-to-all-start.1 = ((bf16[4,160,256]{2,1,0:T(8,128)(2,1)}), bf16[4,160,256]{2,1,0:T(8,128)(2,1)}, u32[]{:S(2)}, u32[]{:S(2)}) async-start(bf16[4,160,256]{2,1,0:T(8,128)(2,1)} %broadcast_in_dim.14), calls=%async_computation.1 | async-start | bytes 655360 | tf_op jit(solution)/shard_map/all_to_all | solution.py:240
  48.0 6.1 %all-to-all-done.1 = bf16[4,160,256]{2,1,0:T(8,128)(2,1)} async-done(((bf16[4,160,256]{2,1,0:T(8,128)(2,1)}), bf16[4,160,256]{2,1,0:T(8,128)(2,1)}, u32[]{:S(2)}, u32[]{:S(2)}) %all-to-all-start.1) | async-done | bytes 327712 | tf_op jit(solution)/shard_map/all_to_all | solution.py:240
  54.0 4.5 %all-gather = bf16[8,160,256]{2,1,0:T(8,128)(2,1)S(1)} all-gather(bf16[4,160,256]{2,1,0:T(8,128)(2,1)} %all-to-all-done.1), channel_id=2, replica_groups=mesh['grp'=2,'seq_0'=16,'seq_1'=4,'seq_2'=2] {'seq_2'}, dimensions={0}, use_global_device_ids=true | all-gather | bytes 983040 | tf_op jit(solution)/shard_map/all_gather | solution.py:262
  58.5 1.2 copy.14
  59.7 2.3 %reshape.38 = bf16[2,4,16,10,256]{4,1,0,3,2:T(4,128)(2,1)} reshape(bf16[8,160,256]{2,0,1:T(8,128)(2,1)} %copy.14) | data formatting | bytes 1310720 | tf_op jit(solution)/shard_map/reshape | solution.py:263
  62.0 2.3 %copy.15 = bf16[16,4,2,10,256]{4,3,2,1,0:T(8,128)(2,1)} copy(bf16[16,4,2,10,256]{4,1,2,3,0:T(4,128)(2,1)} %bitcast.25) | data formatting | bytes 1310720 | tf_op jit(solution)/shard_map/transpose | solution.py:264
  64.3 2.1 %reshape.39.q_ref = bf16[1280,256]{1,0:T(8,128)(2,1)} reshape(bf16[16,4,2,10,256]{4,3,2,1,0:T(8,128)(2,1)} %copy.15) | data formatting | bytes 1310720 | tf_op jit(solution)/shard_map/reshape | solution.py:264
  66.5 1.9 %copy-done.1 = bf16[1280,1280]{1,0:T(8,128)(2,1)S(1)} copy-done((bf16[1280,1280]{1,0:T(8,128)(2,1)S(1)}, bf16[1280,1280]{1,0:T(8,128)(2,1)}, u32[]{:S(2)}) %copy-start.1) | copy-done | bytes 3276824
  68.4 1.9 %copy-done.2 = bf16[1280,1280]{1,0:T(8,128)(2,1)S(1)} copy-done((bf16[1280,1280]{1,0:T(8,128)(2,1)S(1)}, bf16[1280,1280]{1,0:T(8,128)(2,1)}, u32[]{:S(2)}) %copy-start.2) | copy-done | bytes 3276824
  70.3 1.1 copy-done.4
  71.4 16.0 %attend.1 = bf16[8,176,256]{2,1,0:T(8,128)(2,1)S(1)} custom-call(s32[2]{0:T(128)S(1)} %dynamic-slice_reduce_fusion.lengths_ref, f32[20]{0:T(128)S(1)} %copy-done.6, bf16[1280,256]{1,0:T(8,128)(2,1)S(1)} %copy-done.4, bf16[1280,1280]{1,0:T(8,128)(2,1)S(1)} %copy-done.1, bf16[1280,1280]{1,0:T(8,128)(2,1)S(1)} %copy-done.2, ...), custom_call_target="tpu_custom_call" | custom-call | tf_op jit(solution)/shard_map/attend/pallas_call | solution.py:134
  87.4 0.9 copy-done.3
  88.3 4.6 %all-to-all-start.2 = ((bf16[8,176,256]{2,1,0:T(8,128)(2,1)}), bf16[8,176,256]{2,1,0:T(8,128)(2,1)}, u32[]{:S(2)}, u32[]{:S(2)}) async-start(bf16[8,176,256]{2,1,0:T(8,128)(2,1)} %copy-done.3), calls=%async_computation.2 | async-start | bytes 1441792 | tf_op jit(solution)/shard_map/all_to_all | solution.py:280
  92.9 11.7 %all-to-all-done.2.in_ref = bf16[8,176,256]{2,1,0:T(8,128)(2,1)} async-done(((bf16[8,176,256]{2,1,0:T(8,128)(2,1)}), bf16[8,176,256]{2,1,0:T(8,128)(2,1)}, u32[]{:S(2)}, u32[]{:S(2)}) %all-to-all-start.2) | async-done | bytes 720928 | tf_op jit(solution)/shard_map/all_to_all | solution.py:280
  104.6 2.1 %merge.1 = bf16[16,32,128]{2,1,0:T(8,128)(2,1)} custom-call(s32[1]{0:T(128)} %bitcast.1.odd_ref, bf16[8,176,256]{2,1,0:T(8,128)(2,1)} %all-to-all-done.2.in_ref), custom_call_target="tpu_custom_call" | custom-call | tf_op jit(solution)/shard_map/merge/pallas_call | solution.py:226
  106.6 11.6 %all-to-all-start.3 = ((bf16[16,32,128]{2,1,0:T(8,128)(2,1)}), bf16[16,32,128]{2,1,0:T(8,128)(2,1)S(1)}, u32[]{:S(2)}, u32[]{:S(2)}) async-start(bf16[16,32,128]{2,1,0:T(8,128)(2,1)} %merge.1), calls=%async_computation.3 | async-start | bytes 262144 | tf_op jit(solution)/shard_map/all_to_all | solution.py:290
  118.3 11.7 %all-to-all-done.3.in_ref = bf16[16,32,128]{2,1,0:T(8,128)(2,1)S(1)} async-done(((bf16[16,32,128]{2,1,0:T(8,128)(2,1)}), bf16[16,32,128]{2,1,0:T(8,128)(2,1)S(1)}, u32[]{:S(2)}, u32[]{:S(2)}) %all-to-all-start.3) | async-done | bytes 131104 | tf_op jit(solution)/shard_map/all_to_all | solution.py:290
  130.2 17.3 %all_to_all.30 = bf16[16,24,128]{2,1,0:T(8,128)(2,1)S(1)} all-to-all(bf16[16,24,128]{2,1,0:T(8,128)(2,1)S(1)} %broadcast_in_dim.30), channel_id=1, replica_groups=mesh['grp'=2,'seq_0'=16,'seq_1'=4,'seq_2'=2] {'seq_0'}, dimensions={0} | all-to-all | bytes 196608 | tf_op jit(solution)/shard_map/all_to_all | solution.py:240
  147.5 0.8 broadcast_in_dim.32
  148.3 4.2 %all-to-all-start.5 = ((bf16[4,384,128]{2,1,0:T(8,128)(2,1)}), bf16[4,384,128]{2,1,0:T(8,128)(2,1)}, u32[]{:S(2)}, u32[]{:S(2)}) async-start(bf16[4,384,128]{2,1,0:T(8,128)(2,1)} %broadcast_in_dim.32), calls=%async_computation.5 | async-start | bytes 786432 | tf_op jit(solution)/shard_map/all_to_all | solution.py:240
  152.9 1.3 copy.16
  154.2 1.8 %pad.14 = bf16[4,2,8,24,10]{4,3,2,0,1:T(8,128)(2,1)} pad(bf16[4,2,8,20,10]{4,3,2,0,1:T(8,128)(2,1)} %copy.16, bf16[]{:T(256)} %constant.63.clone.1), padding=0_0x0_0x0_0x0_4x0_0 | pad | bytes 56322 | tf_op jit(solution)/shard_map/jit(_pad)/pad | solution.py:305
  156.0 2.7 %all-to-all-done.5 = bf16[4,384,128]{2,1,0:T(8,128)(2,1)} async-done(((bf16[4,384,128]{2,1,0:T(8,128)(2,1)}), bf16[4,384,128]{2,1,0:T(8,128)(2,1)}, u32[]{:S(2)}, u32[]{:S(2)}) %all-to-all-start.5) | async-done | bytes 393248 | tf_op jit(solution)/shard_map/all_to_all | solution.py:240
  158.7 6.5 %all-gather.1 = bf16[8,384,128]{2,1,0:T(8,128)(2,1)S(1)} all-gather(bf16[4,384,128]{2,1,0:T(8,128)(2,1)} %all-to-all-done.5), channel_id=3, replica_groups=mesh['grp'=2,'seq_0'=16,'seq_1'=4,'seq_2'=2] {'seq_2'}, dimensions={0}, use_global_device_ids=true | all-gather | bytes 1179648 | tf_op jit(solution)/shard_map/all_gather | solution.py:302
  165.3 1.0 copy-done.5
  166.7 0.7 copy.17
  (25 shorter events, 1.4 us)
Async XLA Ops:
  0.0 26.8 %copy-start = (bf16[2,640,1280]{2,1,0:T(8,128)(2,1)S(1)}, bf16[2,640,1280]{2,1,0:T(8,128)(2,1)}, u32[]{:S(2)}) copy-start(bf16[2,640,1280]{2,1,0:T(8,128)(2,1)} %param.8) | copy-start | bytes 9830404
  2.3 40.6 %all-to-all-start = ((bf16[16,16,256]{2,1,0:T(8,128)(2,1)}), bf16[16,16,256]{2,1,0:T(8,128)(2,1)S(1)}, u32[]{:S(2)}, u32[]{:S(2)}) async-start(bf16[16,16,256]{2,1,0:T(8,128)(2,1)} %broadcast_in_dim.12), calls=%async_computation | async-start | bytes 262144 | tf_op jit(solution)/shard_map/all_to_all | solution.py:240
  34.5 8.2 %copy-start.9 = (s32[2,128]{1,0:T(2,128)S(1)}, s32[2,128]{1,0:T(2,128)}, u32[]{:S(2)}) copy-start(s32[2,128]{1,0:T(2,128)} %param.14) | copy-start | bytes 3076
  34.5 13.4 %copy-start.8 = (s32[2,128]{1,0:T(2,128)S(1)}, s32[2,128]{1,0:T(2,128)}, u32[]{:S(2)}) copy-start(s32[2,128]{1,0:T(2,128)} %param.15) | copy-start | bytes 3076
  43.6 10.4 %all-to-all-start.1 = ((bf16[4,160,256]{2,1,0:T(8,128)(2,1)}), bf16[4,160,256]{2,1,0:T(8,128)(2,1)}, u32[]{:S(2)}, u32[]{:S(2)}) async-start(bf16[4,160,256]{2,1,0:T(8,128)(2,1)} %broadcast_in_dim.14), calls=%async_computation.1 | async-start | bytes 655360 | tf_op jit(solution)/shard_map/all_to_all | solution.py:240
  47.9 18.5 %copy-start.6 = (f32[20]{0:T(128)S(1)}, f32[20]{0:T(128)}, u32[]{:S(2)}) copy-start(f32[20]{0:T(128)} %slope_ref.1) | copy-start | bytes 244
  66.5 1.9 %copy-start.1 = (bf16[1280,1280]{1,0:T(8,128)(2,1)S(1)}, bf16[1280,1280]{1,0:T(8,128)(2,1)}, u32[]{:S(2)}) copy-start(bf16[1280,1280]{1,0:T(8,128)(2,1)} %convolution_convert_fusion.1.k_ref) | copy-start | bytes 9830404
  68.4 1.9 %copy-start.2 = (bf16[1280,1280]{1,0:T(8,128)(2,1)S(1)}, bf16[1280,1280]{1,0:T(8,128)(2,1)}, u32[]{:S(2)}) copy-start(bf16[1280,1280]{1,0:T(8,128)(2,1)} %convolution_convert_fusion.vt_ref) | copy-start | bytes 9830404
  70.3 1.1 copy-start.4
  87.4 0.9 copy-start.3
  88.3 64.2 %copy-start.7 = (bf16[1280,10]{0,1:T(8,128)(2,1)S(1)}, bf16[1280,10]{0,1:T(8,128)(2,1)}, u32[]{:S(2)}) copy-start(bf16[1280,10]{0,1:T(8,128)(2,1)} %param.12) | copy-start | bytes 76804
  88.3 16.3 %all-to-all-start.2 = ((bf16[8,176,256]{2,1,0:T(8,128)(2,1)}), bf16[8,176,256]{2,1,0:T(8,128)(2,1)}, u32[]{:S(2)}, u32[]{:S(2)}) async-start(bf16[8,176,256]{2,1,0:T(8,128)(2,1)} %copy-done.3), calls=%async_computation.2 | async-start | bytes 1441792 | tf_op jit(solution)/shard_map/all_to_all | solution.py:280
  106.6 23.4 %all-to-all-start.3 = ((bf16[16,32,128]{2,1,0:T(8,128)(2,1)}), bf16[16,32,128]{2,1,0:T(8,128)(2,1)S(1)}, u32[]{:S(2)}, u32[]{:S(2)}) async-start(bf16[16,32,128]{2,1,0:T(8,128)(2,1)} %merge.1), calls=%async_computation.3 | async-start | bytes 262144 | tf_op jit(solution)/shard_map/all_to_all | solution.py:290
  148.3 10.4 %all-to-all-start.5 = ((bf16[4,384,128]{2,1,0:T(8,128)(2,1)}), bf16[4,384,128]{2,1,0:T(8,128)(2,1)}, u32[]{:S(2)}, u32[]{:S(2)}) async-start(bf16[4,384,128]{2,1,0:T(8,128)(2,1)} %broadcast_in_dim.32), calls=%async_computation.5 | async-start | bytes 786432 | tf_op jit(solution)/shard_map/all_to_all | solution.py:240
  165.3 1.0 copy-start.5

commit v2 on v1

--- a/solution.py
+++ b/solution.py
@@ -31,12 +31,52 @@
     return split_rows(peak, PEAK_ROWS) + split_rows(total, STAT_ROWS - PEAK_ROWS)
 
 
+def floor_div(x, n):
+    return (x * (2**19 // n + 1)) >> 19
+
+
+def pair_queries(pair, gathered_ref, rows, columns, beside):
+    near, held, _ = gathered_ref.shape
+    cores = near // beside
+    window = 48
+    span = near * columns
+    first = jnp.minimum((pair * rows // span) * columns // 16, (held - window) // 16)
+    start = pl.multiple_of(first * 16, 16)
+    pieces = [gathered_ref[at, pl.ds(start, window), :] for at in range(near)]
+    shape = (rows, near * window)
+    at = pair * rows + lax.broadcasted_iota(jnp.int32, (rows, 128), 0)
+    far = floor_div(at, span)
+    rest = at - far * span
+    owner = floor_div(rest, columns)
+    column = rest - owner * columns
+    core = owner & (cores - 1)
+    source = core * beside + floor_div(owner, cores)
+    source = source * window + far * columns + column - first * 16
+    source = jnp.concatenate([source] * (near * window // 128), axis=1)
+    picked = (lax.broadcasted_iota(jnp.int32, shape, 1) == source).astype(F32).astype(BF16)
+    queries = jnp.dot(picked, jnp.concatenate(pieces, axis=0), preferred_element_type=F32)
+    return queries.astype(BF16)
+
+
 def attend_kernel(
-    lengths_ref, slope_ref, q_ref, k_ref, vt_ref, dist_ref, msg_ref, stat_ref, *, frame_count, chunks
+    lengths_ref,
+    slope_ref,
+    gathered_ref,
+    k_ref,
+    vt_ref,
+    dist_ref,
+    msg_ref,
+    stat_ref,
+    *,
+    frame_count,
+    chunks,
+    columns,
+    beside,
 ):
     pair = pl.program_id(0)
-    head_size = q_ref.shape[0] // 2
-    tokens = q_ref.shape[1]
+    head_size = k_ref.shape[1] // 2
+    tokens = gathered_ref.shape[2]
+    queries = pair_queries(pair, gathered_ref, 2 * head_size, columns, beside)
     half = tokens // 2
     scale = 1.0 / math.sqrt(head_size)
     lanes = 2 * head_size
@@ -62,8 +102,8 @@
     zeros_half = jnp.zeros((head_size, half), BF16)
     right = jnp.concatenate(
         [
-            jnp.concatenate([q_ref[:head_size, half:], zeros_half], axis=1),
-            jnp.concatenate([zeros_half, q_ref[head_size:, half:]], axis=1),
+            jnp.concatenate([queries[:head_size, half:], zeros_half], axis=1),
+            jnp.concatenate([zeros_half, queries[head_size:, half:]], axis=1),
             floor,
         ],
         axis=0,
@@ -77,7 +117,7 @@
     old_keys = keys_of(0)
     for side in range(2):
         head = 2 * pair + side
-        own = q_ref[side * head_size : (side + 1) * head_size, :]
+        own = queries[side * head_size : (side + 1) * head_size, :]
         right = jnp.concatenate([own, zeros, floor] if side == 0 else [zeros, own, floor], axis=0)
         old_peak, old_weights = weigh(old_keys, right)
         old_sum = jnp.dot(
@@ -126,28 +166,31 @@
             msg_ref[chunk, chunk_rows:, :] = jnp.concatenate(rows, axis=0).astype(BF16)
 
 
-def attend(lengths, slope, queries, keys, values_t, dist, frame_count, chunks):
-    width, tokens = queries.shape
+def attend(lengths, slope, gathered, keys, values_t, dist, frame_count, columns, beside):
+    near, _, tokens = gathered.shape
+    rows, width = keys.shape
     head_count = slope.shape[0]
     pair_rows = 2 * (width // head_count)
-    rows = keys.shape[0]
+    keys, values_t = (pltpu.with_memory_space_constraint(x, pltpu.HBM) for x in (keys, values_t))
     return pl.pallas_call(
-        functools.partial(attend_kernel, frame_count=frame_count, chunks=chunks),
+        functools.partial(
+            attend_kernel, frame_count=frame_count, chunks=near, columns=columns, beside=beside
+        ),
         grid=(head_count // 2,),
         in_specs=[
             pl.BlockSpec(memory_space=pltpu.SMEM),
             pl.BlockSpec(memory_space=pltpu.SMEM),
-            pl.BlockSpec((pair_rows, tokens), lambda p: (p, 0)),
+            pl.BlockSpec(gathered.shape, lambda p: (0, 0, 0)),
             pl.BlockSpec((rows, pair_rows), lambda p: (0, p)),
             pl.BlockSpec((pair_rows, rows), lambda p: (p, 0)),
             pl.BlockSpec(dist.shape, lambda p: (0, 0)),
         ],
-        out_specs=pl.BlockSpec((chunks, width // chunks + 16, tokens), lambda p: (0, 0, 0)),
-        out_shape=jax.ShapeDtypeStruct((chunks, width // chunks + 16, tokens), BF16),
+        out_specs=pl.BlockSpec((near, width // near + 16, tokens), lambda p: (0, 0, 0)),
+        out_shape=jax.ShapeDtypeStruct((near, width // near + 16, tokens), BF16),
         scratch_shapes=[pltpu.VMEM((head_count, 8, tokens), F32)],
         compiler_params=pltpu.CompilerParams(vmem_limit_bytes=40 << 20),
         name="attend",
-    )(lengths, slope, queries, keys, values_t, dist)
+    )(lengths, slope, gathered, keys, values_t, dist)
 
 
 def merge_kernel(odd_ref, in_ref, out_ref):
@@ -259,9 +302,7 @@
     padded = jnp.pad(own_queries, ((0, 16 - columns), (0, 0)))
     queries = spread(padded, "seq_0")[:, :columns]
     queries = spread(queries.reshape(across * columns, tokens), "seq_1")
-    queries = lax.all_gather(queries, "seq_2")
-    queries = queries.reshape(cores, beside, across, columns, tokens)
-    queries = queries.transpose(2, 1, 0, 3, 4).reshape(width, tokens)
+    queries = lax.all_gather(queries, "seq_2").reshape(near, across * columns, tokens)
 
     frame_rows = frames.reshape(step_count * frame_count, width)
     keys = jnp.dot(frame_rows, w_keyval[:, :width], preferred_element_type=F32).astype(BF16)
@@ -276,10 +317,20 @@
     dist = jnp.pad(dist, ((0, 6), (0, 0)))
     own_lengths = lax.dynamic_slice(lengths, (0, own_index), (step_count, 1)).reshape(step_count)
 
-    message = attend(own_lengths, head_slope, queries, keys, values_t, dist, frame_count, near)
-    message = lax.all_to_all(message, ("seq_1", "seq_2"), 0, 0)
     odd = (lax.axis_index(("seq_1", "seq_2")) % 2).astype(jnp.int32).reshape(1)
     piece = 2 * width // devices
+    at = (lax.axis_index("seq_0") % (across // 2)) * piece
+    bound = (SLAB - at % SLAB).astype(jnp.int32).reshape(1)
+    weights = w_output.reshape(beside, cores, across // 2, piece, columns)
+    weights = jnp.pad(weights, ((0, 0), (0, 0), (0, 0), (0, 24 - piece), (0, 0)))
+    weights = weights.transpose(1, 0, 2, 3, 4).reshape(near, across // 2 * 24, columns)
+    queries, weights, odd, bound, dist, own_lengths = lax.optimization_barrier(
+        (queries, weights, odd, bound, dist, own_lengths)
+    )
+    message = attend(
+        own_lengths, head_slope, queries, keys, values_t, dist, frame_count, columns, beside
+    )
+    message = lax.all_to_all(message, ("seq_1", "seq_2"), 0, 0)
     message = whole(
         merge_kernel,
         jax.ShapeDtypeStruct((across, SLAB, tokens // 2), BF16),
@@ -288,8 +339,6 @@
         "merge",
     )
     message = lax.all_to_all(message, "seq_0", 0, 0)
-    at = (lax.axis_index("seq_0") % (across // 2)) * piece
-    bound = (SLAB - at % SLAB).astype(jnp.int32).reshape(1)
     context = whole(
         functools.partial(finish_kernel, piece=piece),
         jax.ShapeDtypeStruct((24, tokens // 2), BF16),
@@ -301,9 +350,6 @@
     context = spread(context.reshape(across * 24, tokens // 2), "seq_1")
     context = lax.all_gather(context, "seq_2")
     context = context.reshape(near, 2, across // 2 * 24, tokens // 2)
-    weights = w_output.reshape(beside, cores, across // 2, piece, columns)
-    weights = jnp.pad(weights, ((0, 0), (0, 0), (0, 0), (0, 24 - piece), (0, 0)))
-    weights = weights.transpose(1, 0, 2, 3, 4).reshape(near, across // 2 * 24, columns)
     return whole(
         project_kernel,
         jax.ShapeDtypeStruct((step_count, query_rows, columns), BF16),

time: 168 us -> 153 us (0.911)
  blocking collectives: 28.3 us -> 74.4 us
  waiting for transfers between devices: 32.2 us -> 6.09 us
  starting transfers between devices: 49.3 us -> 28.8 us
  local copies, waits for them, and re-layouts: 21.5 us -> 6.93 us
    all_to_all x0 -> x2, blocking collectives: none -> 37.7 us  [the longest x1 23.2 us: local(): message = lax.all_to_all(message, 'seq_0', 0, 0)]
    all_to_all x2 -> x0, waiting for transfers between devices: 23.4 us -> none  [the longest x1 11.7 us: local(): message = lax.all_to_all(message, 'seq_0', 0, 0)]
    all_to_all x2 -> x0, starting transfers between devices: 16.2 us -> none  [the longest x1 11.6 us: local(): message = lax.all_to_all(message, 'seq_0', 0, 0)]
    all_to_all x1 -> x2, blocking collectives: 17.3 us -> 25.9 us  [spread(): return lax.all_to_all(copies, axis, 0, 0)]
    unnamed x20 -> x12, local copies, waits for them, and re-layouts: 6.84 us -> 0.02 us
    reshape x2 -> x0, local copies, waits for them, and re-layouts: 4.49 us -> none  [the longest x1 2.35 us: local(): queries = queries.reshape(cores, beside, across, columns, tokens)]
    all_to_all x3 -> x2, starting transfers between devices: 33 us -> 28.8 us  [spread(): return lax.all_to_all(copies, axis, 0, 0)]
    all_to_all x3 -> x2, waiting for transfers between devices: 8.79 us -> 6.09 us  [spread(): return lax.all_to_all(copies, axis, 0, 0)]
  transfers between devices with their start and end apart: 5 -> 2, of which waited for: 4 -> 1; matrix products, arithmetic and copies ran while one was open for 12% -> 13% of each run, Pallas kernels for 0% -> 0%
where the time goes in v2:
time: 153 us
  blocking collectives  74.4 us (49%)
  starting transfers between devices  28.8 us (19%)
  Pallas kernels  18.8 us (12%)
  matrix products  17.3 us (11%)
  local copies, waits for them, and re-layouts  6.93 us (5%)
  waiting for transfers between devices  6.09 us (4%)
    all_to_all x2, starting transfers between devices, spread(): return lax.all_to_all(copies, axis, 0, 0)  28.8 us
    all_to_all x2, blocking collectives, spread(): return lax.all_to_all(copies, axis, 0, 0)  25.9 us
    all_to_all x1, blocking collectives, local(): message = lax.all_to_all(message, 'seq_0', 0, 0)  23.2 us
    pallas_call x1, Pallas kernels, attend(): pl.pallas_call(functools.partial(attend_kernel, frame_count=frame_count,...  17.9 us
    all_to_all x1, blocking collectives, local(): message = lax.all_to_all(message, ('seq_1', 'seq_2'), 0, 0)  14.5 us
    dot_general x1, matrix products, local(): lax.dot_general(w_keyval[:, width:], frame_rows, (((0,), (1,)), ((), ()))...  8.12 us
    dot_general x1, matrix products, local(): jnp.dot(frame_rows, w_keyval[:, :width], preferred_element_type=F32)  7.71 us
    all_gather x1, blocking collectives, local(): context = lax.all_gather(context, 'seq_2')  6.33 us
  transfers between devices with their start and end apart: 2, of which 1 were waited for; matrix products, arithmetic and copies ran while one was open for 13% of the time, Pallas kernels for 0%

profile of v2, /device:TPU:33, one launch (start us, length us, event | category | flops | bytes accessed | tf_op | source)
XLA Modules:
  0.0 152.5 jit_solution(7319587309722950567)
XLA Ops:
  0.0 0.0 copy-start
  0.0 1.5 convolution_convert_fusion.2
  1.5 0.1 pad.12
  1.6 0.7 broadcast_in_dim.12
  2.3 24.5 %all-to-all-start = ((bf16[16,16,256]{2,1,0:T(8,128)(2,1)}), bf16[16,16,256]{2,1,0:T(8,128)(2,1)}, u32[]{:S(2)}, u32[]{:S(2)}) async-start(bf16[16,16,256]{2,1,0:T(8,128)(2,1)} %broadcast_in_dim.12), calls=%async_computation | async-start | bytes 262144 | tf_op jit(solution)/shard_map/all_to_all | solution.py:283
  26.8 0.0 copy-done
  26.8 8.1 %convolution_convert_fusion.vt_ref = bf16[1280,1280]{1,0:T(8,128)(2,1)} fusion(bf16[1280,1280]{1,0:T(8,128)(2,1)S(1)} %bitcast.19, bf16[1280,2560]{1,0:T(8,128)(2,1)} %param.11), kind=kOutput, calls=%fused_computation | convolution fusion | flops 4195942400 | bytes 9830400 | tf_op jit(solution)/shard_map/dot_general | solution.py:309
  34.9 7.7 %convolution_convert_fusion.1.k_ref = bf16[1280,1280]{1,0:T(8,128)(2,1)} fusion(bf16[1280,1280]{1,0:T(8,128)(2,1)S(1)} %bitcast.18, bf16[1280,2560]{1,0:T(8,128)(2,1)} %param.11), kind=kOutput, calls=%fused_computation.1 | convolution fusion | flops 4195942400 | bytes 9830400 | tf_op jit(solution)/shard_map/dot_general | solution.py:308
  42.6 0.0 copy-done.3
  42.6 0.4 reshape.33
  43.0 1.3 copy.13
  44.3 1.9 %pad.13 = bf16[4,2,8,24,10]{4,3,2,0,1:T(8,128)(2,1)} pad(bf16[4,2,8,20,10]{4,3,2,0,1:T(8,128)(2,1)} %copy.13, bf16[]{:T(256)} %constant.51.clone.1), padding=0_0x0_0x0_0x0_4x0_0 | pad | bytes 56322 | tf_op jit(solution)/shard_map/jit(_pad)/pad | solution.py:325
  46.2 0.2 dynamic-slice_reduce_fusion.lengths_ref
  46.4 0.0 all-to-all-done
  46.4 0.9 broadcast_in_dim.13
  47.3 0.7 broadcast_in_dim.14
  48.1 4.3 %all-to-all-start.1 = ((bf16[4,160,256]{2,1,0:T(8,128)(2,1)}), bf16[4,160,256]{2,1,0:T(8,128)(2,1)}, u32[]{:S(2)}, u32[]{:S(2)}) async-start(bf16[4,160,256]{2,1,0:T(8,128)(2,1)} %broadcast_in_dim.14), calls=%async_computation.1 | async-start | bytes 655360 | tf_op jit(solution)/shard_map/all_to_all | solution.py:283
  52.4 6.1 %all-to-all-done.1 = bf16[4,160,256]{2,1,0:T(8,128)(2,1)} async-done(((bf16[4,160,256]{2,1,0:T(8,128)(2,1)}), bf16[4,160,256]{2,1,0:T(8,128)(2,1)}, u32[]{:S(2)}, u32[]{:S(2)}) %all-to-all-start.1) | async-done | bytes 327712 | tf_op jit(solution)/shard_map/all_to_all | solution.py:283
  58.5 4.5 %all-gather.gathered_ref = bf16[8,160,256]{2,1,0:T(8,128)(2,1)S(1)} all-gather(bf16[4,160,256]{2,1,0:T(8,128)(2,1)} %all-to-all-done.1), channel_id=2, replica_groups=mesh['grp'=2,'seq_0'=16,'seq_1'=4,'seq_2'=2] {'seq_2'}, dimensions={0}, use_global_device_ids=true | all-gather | bytes 983040 | tf_op jit(solution)/shard_map/all_gather | solution.py:305
  62.9 17.9 %attend.1 = bf16[8,176,256]{2,1,0:T(8,128)(2,1)S(1)} custom-call(s32[2]{0:T(128)S(1)} %dynamic-slice_reduce_fusion.lengths_ref, f32[20]{0:T(128)S(1)} %copy-done.2, bf16[8,160,256]{2,1,0:T(8,128)(2,1)S(1)} %all-gather.gathered_ref, bf16[1280,1280]{1,0:T(8,128)(2,1)} %convolution_convert_fusion.1.k_ref, bf16[1280,1280]{1,0:T(8,128)(2,1)} %convolution_convert_fusion.vt_ref, ...), custom_call_target="tpu_custom_call" | custom-call | tf_op jit(solution)/shard_map/attend/pallas_call | solution.py:175
  80.9 0.0 copy-start.1
  80.9 14.5 %all_to_all.30.in_ref = bf16[8,176,256]{2,1,0:T(8,128)(2,1)S(1)} all-to-all(bf16[8,176,256]{2,1,0:T(8,128)(2,1)S(1)} %attend.1), channel_id=1, replica_groups=mesh['grp'=2,'seq_0'=16,'seq_1'=4,'seq_2'=2] {'seq_1','seq_2'}, dimensions={0} | all-to-all | bytes 1441792 | tf_op jit(solution)/shard_map/all_to_all | solution.py:333
  95.4 0.3 merge.1
  95.7 23.2 %all_to_all.31.in_ref = bf16[16,32,128]{2,1,0:T(8,128)(2,1)S(1)} all-to-all(bf16[16,32,128]{2,1,0:T(8,128)(2,1)S(1)} %merge.1), channel_id=1, replica_groups=mesh['grp'=2,'seq_0'=16,'seq_1'=4,'seq_2'=2] {'seq_0'}, dimensions={0} | all-to-all | bytes 262144 | tf_op jit(solution)/shard_map/all_to_all | solution.py:341
  118.9 0.1 finish.1
  119.0 17.3 %all_to_all.32 = bf16[16,24,128]{2,1,0:T(8,128)(2,1)S(1)} all-to-all(bf16[16,24,128]{2,1,0:T(8,128)(2,1)S(1)} %broadcast_in_dim.30), channel_id=1, replica_groups=mesh['grp'=2,'seq_0'=16,'seq_1'=4,'seq_2'=2] {'seq_0'}, dimensions={0} | all-to-all | bytes 196608 | tf_op jit(solution)/shard_map/all_to_all | solution.py:283
  136.3 0.1 broadcast_in_dim.32
  136.4 8.7 %all_to_all.33 = bf16[4,384,128]{2,1,0:T(8,128)(2,1)S(1)} all-to-all(bf16[4,384,128]{2,1,0:T(8,128)(2,1)S(1)} %broadcast_in_dim.32), channel_id=1, replica_groups=mesh['grp'=2,'seq_0'=16,'seq_1'=4,'seq_2'=2] {'seq_1'}, dimensions={0} | all-to-all | bytes 786432 | tf_op jit(solution)/shard_map/all_to_all | solution.py:283
  145.0 6.3 %all-gather.1 = bf16[8,384,128]{2,1,0:T(8,128)(2,1)S(1)} all-gather(bf16[4,384,128]{2,1,0:T(8,128)(2,1)S(1)} %all_to_all.33), channel_id=3, replica_groups=mesh['grp'=2,'seq_0'=16,'seq_1'=4,'seq_2'=2] {'seq_2'}, dimensions={0}, use_global_device_ids=true | all-gather | bytes 1179648 | tf_op jit(solution)/shard_map/all_gather | solution.py:351
  151.3 0.0 copy-done.1
  151.3 0.5 project.1
  151.8 0.7 copy.14
  (10 shorter events, 0.0 us)
Async XLA Ops:
  0.0 26.8 %copy-start = (bf16[2,640,1280]{2,1,0:T(8,128)(2,1)S(1)}, bf16[2,640,1280]{2,1,0:T(8,128)(2,1)}, u32[]{:S(2)}) copy-start(bf16[2,640,1280]{2,1,0:T(8,128)(2,1)} %param.8) | copy-start | bytes 9830404
  2.3 44.1 %all-to-all-start = ((bf16[16,16,256]{2,1,0:T(8,128)(2,1)}), bf16[16,16,256]{2,1,0:T(8,128)(2,1)}, u32[]{:S(2)}, u32[]{:S(2)}) async-start(bf16[16,16,256]{2,1,0:T(8,128)(2,1)} %broadcast_in_dim.12), calls=%async_computation | async-start | bytes 262144 | tf_op jit(solution)/shard_map/all_to_all | solution.py:283
  34.9 7.7 %copy-start.3 = (bf16[1280,10]{0,1:T(8,128)(2,1)S(1)}, bf16[1280,10]{0,1:T(8,128)(2,1)}, u32[]{:S(2)}) copy-start(bf16[1280,10]{0,1:T(8,128)(2,1)} %param.12) | copy-start | bytes 76804
  34.9 11.3 %copy-start.5 = (s32[2,128]{1,0:T(2,128)S(1)}, s32[2,128]{1,0:T(2,128)}, u32[]{:S(2)}) copy-start(s32[2,128]{1,0:T(2,128)} %param.14) | copy-start | bytes 3076
  34.9 17.4 %copy-start.4 = (s32[2,128]{1,0:T(2,128)S(1)}, s32[2,128]{1,0:T(2,128)}, u32[]{:S(2)}) copy-start(s32[2,128]{1,0:T(2,128)} %param.15) | copy-start | bytes 3076
  42.6 20.3 %copy-start.2 = (f32[20]{0:T(128)S(1)}, f32[20]{0:T(128)}, u32[]{:S(2)}) copy-start(f32[20]{0:T(128)} %slope_ref.1) | copy-start | bytes 244
  48.1 10.4 %all-to-all-start.1 = ((bf16[4,160,256]{2,1,0:T(8,128)(2,1)}), bf16[4,160,256]{2,1,0:T(8,128)(2,1)}, u32[]{:S(2)}, u32[]{:S(2)}) async-start(bf16[4,160,256]{2,1,0:T(8,128)(2,1)} %broadcast_in_dim.14), calls=%async_computation.1 | async-start | bytes 655360 | tf_op jit(solution)/shard_map/all_to_all | solution.py:283
  80.9 70.5 %copy-start.1 = (bf16[4,2,8,24,10]{4,3,2,0,1:T(8,128)(2,1)S(1)}, bf16[4,2,8,24,10]{4,3,2,0,1:T(8,128)(2,1)}, u32[]{:S(2)}) copy-start(bf16[4,2,8,24,10]{4,3,2,0,1:T(8,128)(2,1)} %pad.13) | copy-start | bytes 92164

commit v3 on v2

--- a/solution.py
+++ b/solution.py
@@ -15,6 +15,8 @@
 SLAB = 32
 PEAK_ROWS = 3
 STAT_ROWS = 5
+PAIRS = 2
+AHEAD = 3
 LOG2E = math.log2(math.e)
 
 
@@ -35,9 +37,8 @@
     return (x * (2**19 // n + 1)) >> 19
 
 
-def pair_queries(pair, gathered_ref, rows, columns, beside):
+def pair_queries(pair, gathered_ref, rows, columns):
     near, held, _ = gathered_ref.shape
-    cores = near // beside
     window = 48
     span = near * columns
     first = jnp.minimum((pair * rows // span) * columns // 16, (held - window) // 16)
@@ -49,9 +50,7 @@
     rest = at - far * span
     owner = floor_div(rest, columns)
     column = rest - owner * columns
-    core = owner & (cores - 1)
-    source = core * beside + floor_div(owner, cores)
-    source = source * window + far * columns + column - first * 16
+    source = owner * window + far * columns + column - first * 16
     source = jnp.concatenate([source] * (near * window // 128), axis=1)
     picked = (lax.broadcasted_iota(jnp.int32, shape, 1) == source).astype(F32).astype(BF16)
     queries = jnp.dot(picked, jnp.concatenate(pieces, axis=0), preferred_element_type=F32)
@@ -67,75 +66,86 @@
     dist_ref,
     msg_ref,
     stat_ref,
+    query_ref,
     *,
     frame_count,
     chunks,
     columns,
-    beside,
+    head_size,
 ):
-    pair = pl.program_id(0)
-    head_size = k_ref.shape[1] // 2
+    step, last = pl.program_id(0), pl.num_programs(0) - 1
+    lanes = 2 * head_size
+    pairs = k_ref.shape[1] // lanes
     tokens = gathered_ref.shape[2]
-    queries = pair_queries(pair, gathered_ref, 2 * head_size, columns, beside)
     half = tokens // 2
     scale = 1.0 / math.sqrt(head_size)
-    lanes = 2 * head_size
-
-    def keys_of(block):
-        keys = k_ref[block * frame_count : (block + 1) * frame_count, :]
-        row = lax.broadcasted_iota(jnp.int32, (frame_count, lanes), 0)
-        lane = lax.broadcasted_iota(jnp.int32, (frame_count, lanes), 1)
-        invalid = jnp.logical_and(row >= lengths_ref[block], lane == 0)
-        return jnp.concatenate([keys, jnp.where(invalid, 1.0, 0.0).astype(BF16)], axis=1)
-
+
+    def find_queries(step_at, slot):
+        for pair in range(pairs):
+            query_ref[slot, pair] = pair_queries(
+                step_at * pairs + pair, gathered_ref, lanes, columns
+            )
+
+    @pl.when(step == 0)
+    def _():
+        find_queries(0, 0)
+
+    row = lax.broadcasted_iota(jnp.int32, (frame_count, lanes), 0)
+    lane = lax.broadcasted_iota(jnp.int32, (frame_count, lanes), 1)
+    invalid = [
+        jnp.where(jnp.logical_and(row >= lengths_ref[block], lane == 0), 1.0, 0.0).astype(BF16)
+        for block in range(2)
+    ]
     floor_row = lax.broadcasted_iota(jnp.int32, (lanes, tokens), 0)
     floor = jnp.where(floor_row == 0, -1e30, 0.0).astype(BF16)
-
-    def weigh(keys, right):
-        scores = jnp.dot(keys, right, preferred_element_type=F32)
-        peak = jnp.max(scores, axis=0, keepdims=True)
-        weights = jnp.exp2((scores - peak) * (scale * LOG2E)).astype(BF16)
-        return peak * scale, weights
-
     ones = jnp.ones((16, frame_count), BF16)
     zeros = jnp.zeros((head_size, tokens), BF16)
     zeros_half = jnp.zeros((head_size, half), BF16)
-    right = jnp.concatenate(
-        [
-            jnp.concatenate([queries[:head_size, half:], zeros_half], axis=1),
-            jnp.concatenate([zeros_half, queries[head_size:, half:]], axis=1),
-            floor,
-        ],
-        axis=0,
-    )
-    new_peak, new_weights = weigh(keys_of(1), right)
-    new_sum = jnp.dot(
-        jnp.concatenate([vt_ref[:, frame_count:], ones], axis=0),
-        new_weights,
-        preferred_element_type=F32,
-    )
-    old_keys = keys_of(0)
-    for side in range(2):
-        head = 2 * pair + side
-        own = queries[side * head_size : (side + 1) * head_size, :]
-        right = jnp.concatenate([own, zeros, floor] if side == 0 else [zeros, own, floor], axis=0)
-        old_peak, old_weights = weigh(old_keys, right)
-        old_sum = jnp.dot(
-            jnp.concatenate(
-                [vt_ref[side * head_size : (side + 1) * head_size, :frame_count], ones], axis=0
-            ),
-            old_weights,
+
+    units = [(pair, part) for pair in range(pairs) for part in range(3)]
+
+    def score(pair, part):
+        block = 1 if part == 0 else 0
+        keys = k_ref[block * frame_count : (block + 1) * frame_count, pair * lanes : (pair + 1) * lanes]
+        first = query_ref[step % 2, pair, :head_size, :]
+        second = query_ref[step % 2, pair, head_size:, :]
+        if part == 0:
+            rows = [
+                jnp.concatenate([first[:, half:], zeros_half], axis=1),
+                jnp.concatenate([zeros_half, second[:, half:]], axis=1),
+            ]
+        else:
+            rows = [first, zeros] if part == 1 else [zeros, second]
+        return jnp.dot(
+            jnp.concatenate([keys, invalid[block]], axis=1),
+            jnp.concatenate(rows + [floor], axis=0),
             preferred_element_type=F32,
         )
+
+    def weigh(pair, part, scores):
+        peak = jnp.max(scores, axis=0, keepdims=True)
+        weights = jnp.exp2((scores - peak) * (scale * LOG2E)).astype(BF16)
+        top = pair * lanes
+        if part == 0:
+            values = vt_ref[top : top + lanes, frame_count:]
+        else:
+            start = top + (part - 1) * head_size
+            values = vt_ref[start : start + head_size, :frame_count]
+        values = jnp.concatenate([values, ones], axis=0)
+        return peak * scale, jnp.dot(values, weights, preferred_element_type=F32)
+
+    def emit(pair, side, new, old):
+        head = (step * pairs + pair) * 2 + side
+        (new_peak, new_sum), (old_peak, old_sum) = new, old
         slope = slope_ref[head]
+        late = slice(side * half, (side + 1) * half)
         old_peak = old_peak - slope * dist_ref[0:1, :]
-        late_peak = new_peak[:, side * half : (side + 1) * half] - slope * dist_ref[1:2, half:]
-        late = slice(side * half, (side + 1) * half)
+        late_peak = new_peak[:, late] - slope * dist_ref[1:2, half:]
         top = jnp.maximum(old_peak[:, half:], late_peak)
         old_factor = jnp.exp(old_peak[:, half:] - top)
         new_factor = jnp.exp(late_peak - top)
         old_total = old_sum[head_size : head_size + 1, :]
-        new_total = new_sum[2 * head_size : 2 * head_size + 1, late]
+        new_total = new_sum[lanes : lanes + 1, late]
         second = (
             old_sum[:head_size, half:] * old_factor
             + new_sum[side * head_size : (side + 1) * head_size, late] * new_factor
@@ -153,9 +163,20 @@
             [old_total[:, :half], old_total[:, half:] * old_factor + new_total * new_factor], axis=1
         )
 
-    @pl.when(pair == pl.num_programs(0) - 1)
+    ahead = [score(*units[at]) for at in range(AHEAD)]
+    done = {}
+    for at, (pair, part) in enumerate(units):
+        if at + AHEAD < len(units):
+            ahead.append(score(*units[at + AHEAD]))
+        if at == 1:
+            find_queries(jnp.minimum(step + 1, last), 1 - step % 2)
+        done[part] = weigh(pair, part, ahead[at])
+        ahead[at] = None
+        if part > 0:
+            emit(pair, part - 1, done[0], done[part])
+
+    @pl.when(step == last)
     def _():
-        heads = stat_ref.shape[0]
         chunk_rows = msg_ref.shape[1] - 16
         for chunk in range(chunks):
             first = chunk * chunk_rows // head_size
@@ -166,28 +187,36 @@
             msg_ref[chunk, chunk_rows:, :] = jnp.concatenate(rows, axis=0).astype(BF16)
 
 
-def attend(lengths, slope, gathered, keys, values_t, dist, frame_count, columns, beside):
+def attend(lengths, slope, gathered, keys, values_t, dist, frame_count, columns):
     near, _, tokens = gathered.shape
     rows, width = keys.shape
     head_count = slope.shape[0]
-    pair_rows = 2 * (width // head_count)
+    head_size = width // head_count
+    step_rows = PAIRS * 2 * head_size
     keys, values_t = (pltpu.with_memory_space_constraint(x, pltpu.HBM) for x in (keys, values_t))
     return pl.pallas_call(
         functools.partial(
-            attend_kernel, frame_count=frame_count, chunks=near, columns=columns, beside=beside
+            attend_kernel,
+            frame_count=frame_count,
+            chunks=near,
+            columns=columns,
+            head_size=head_size,
         ),
-        grid=(head_count // 2,),
+        grid=(width // step_rows,),
         in_specs=[
             pl.BlockSpec(memory_space=pltpu.SMEM),
             pl.BlockSpec(memory_space=pltpu.SMEM),
             pl.BlockSpec(gathered.shape, lambda p: (0, 0, 0)),
-            pl.BlockSpec((rows, pair_rows), lambda p: (0, p)),
-            pl.BlockSpec((pair_rows, rows), lambda p: (p, 0)),
+            pl.BlockSpec((rows, step_rows), lambda p: (0, p)),
+            pl.BlockSpec((step_rows, rows), lambda p: (p, 0)),
             pl.BlockSpec(dist.shape, lambda p: (0, 0)),
         ],
         out_specs=pl.BlockSpec((near, width // near + 16, tokens), lambda p: (0, 0, 0)),
         out_shape=jax.ShapeDtypeStruct((near, width // near + 16, tokens), BF16),
-        scratch_shapes=[pltpu.VMEM((head_count, 8, tokens), F32)],
+        scratch_shapes=[
+            pltpu.VMEM((head_count, 8, tokens), F32),
+            pltpu.VMEM((2, PAIRS, 2 * head_size, tokens), BF16),
+        ],
         compiler_params=pltpu.CompilerParams(vmem_limit_bytes=40 << 20),
         name="attend",
     )(lengths, slope, gathered, keys, values_t, dist)
@@ -301,13 +330,14 @@
     ).astype(BF16)
     padded = jnp.pad(own_queries, ((0, 16 - columns), (0, 0)))
     queries = spread(padded, "seq_0")[:, :columns]
-    queries = spread(queries.reshape(across * columns, tokens), "seq_1")
-    queries = lax.all_gather(queries, "seq_2").reshape(near, across * columns, tokens)
+    queries, late_frames = lax.optimization_barrier((queries, frames))
+    queries = spread(queries.reshape(across * columns, tokens), SEQ[1:])
 
     frame_rows = frames.reshape(step_count * frame_count, width)
     keys = jnp.dot(frame_rows, w_keyval[:, :width], preferred_element_type=F32).astype(BF16)
+    late_rows = late_frames.reshape(step_count * frame_count, width)
     values_t = lax.dot_general(
-        w_keyval[:, width:], frame_rows, (((0,), (1,)), ((), ())), preferred_element_type=F32
+        w_keyval[:, width:], late_rows, (((0,), (1,)), ((), ())), preferred_element_type=F32
     ).astype(BF16)
 
     slot_place = ((own_index + 1) % devices).astype(F32)
@@ -328,7 +358,7 @@
         (queries, weights, odd, bound, dist, own_lengths)
     )
     message = attend(
-        own_lengths, head_slope, queries, keys, values_t, dist, frame_count, columns, beside
+        own_lengths, head_slope, queries, keys, values_t, dist, frame_count, columns
     )
     message = lax.all_to_all(message, ("seq_1", "seq_2"), 0, 0)
     message = whole(

time: 153 us -> 140 us (0.915)
  Pallas kernels: 18.8 us -> 11.3 us
  blocking collectives: 74.4 us -> 67.5 us
  starting transfers between devices: 28.8 us -> 32.8 us
  waiting for transfers between devices: 6.09 us -> 3.12 us
    pallas_call x1, Pallas kernels: 17.9 us -> 10.3 us  [attend(): pl.pallas_call(functools.partial(attend_kernel, frame_count=frame_count,...]
    all_gather x1 -> x0, blocking collectives: 4.45 us -> none  [local(): lax.all_gather(queries, 'seq_2').reshape(near, across * columns, tokens)]
    all_to_all x2, starting transfers between devices: 28.8 us -> 32.8 us  [spread(): return lax.all_to_all(copies, axis, 0, 0)]
    all_to_all x1, blocking collectives: 23.2 us -> 20.1 us  [local(): message = lax.all_to_all(message, 'seq_0', 0, 0)]
    all_to_all x2, waiting for transfers between devices: 6.09 us -> 3.12 us  [spread(): return lax.all_to_all(copies, axis, 0, 0)]
  transfers between devices with their start and end apart: 2 -> 2, of which waited for: 1 -> 2; matrix products, arithmetic and copies ran while one was open for 13% -> 14% of each run, Pallas kernels for 0% -> 0%
where the time goes in v3:
time: 140 us; the launch traced here: 139 us
  blocking collectives  67.5 us (48%)
  starting transfers between devices  32.8 us (23%)
  matrix products  17.3 us (12%)
  Pallas kernels  11.3 us (8%)
  local copies, waits for them, and re-layouts  7.06 us (5%)
  waiting for transfers between devices  3.12 us (2%)
    all_to_all x2, starting transfers between devices, spread(): return lax.all_to_all(copies, axis, 0, 0)  32.8 us
    all_to_all x2, blocking collectives, spread(): return lax.all_to_all(copies, axis, 0, 0)  25.9 us
    all_to_all x1, blocking collectives, local(): message = lax.all_to_all(message, 'seq_0', 0, 0)  20.1 us
    all_to_all x1, blocking collectives, local(): message = lax.all_to_all(message, ('seq_1', 'seq_2'), 0, 0)  15.1 us
    pallas_call x1, Pallas kernels, attend(): pl.pallas_call(functools.partial(attend_kernel, frame_count=frame_count,...  10.3 us
    dot_general x1, matrix products, local(): lax.dot_general(w_keyval[:, width:], late_rows, (((0,), (1,)), ((), ())),...  8.11 us
    dot_general x1, matrix products, local(): jnp.dot(frame_rows, w_keyval[:, :width], preferred_element_type=F32)  7.69 us
    all_gather x1, blocking collectives, local(): context = lax.all_gather(context, 'seq_2')  6.33 us
  transfers between devices with their start and end apart: 2, of which 2 were waited for; matrix products, arithmetic and copies ran while one was open for 14% of the time, Pallas kernels for 0%

profile of v3, /device:TPU:33, one launch (start us, length us, event | category | flops | bytes accessed | tf_op | source)
XLA Modules:
  0.0 139.2 jit_solution(7851515391196375323)
XLA Ops:
  0.0 1.5 %convolution_convert_fusion.2 = bf16[10,256]{1,0:T(8,128)(2,1)S(1)} fusion(bf16[1280,10]{0,1:T(8,128)(2,1)} %param.10, bf16[256,1280]{1,0:T(8,128)(2,1)} %bitcast.25), kind=kOutput, calls=%fused_computation.5 | convolution fusion | flops 6556160 | bytes 686080 | tf_op jit(solution)/shard_map/dot_general | solution.py:325
  1.5 0.1 pad.12
  1.6 0.7 broadcast_in_dim.12
  2.2 24.5 %all-to-all-start = ((bf16[16,16,256]{2,1,0:T(8,128)(2,1)}), bf16[16,16,256]{2,1,0:T(8,128)(2,1)}, u32[]{:S(2)}, u32[]{:S(2)}) async-start(bf16[16,16,256]{2,1,0:T(8,128)(2,1)} %broadcast_in_dim.12), calls=%async_computation | async-start | bytes 262144 | tf_op jit(solution)/shard_map/all_to_all | solution.py:312
  26.8 0.0 copy-start.3
  26.8 0.0 copy-start.5
  26.8 0.0 copy-start.4
  26.8 7.7 %convolution_convert_fusion.1.k_ref = bf16[1280,1280]{1,0:T(8,128)(2,1)} fusion(bf16[1280,1280]{1,0:T(8,128)(2,1)S(1)} %bitcast.21, bf16[1280,2560]{1,0:T(8,128)(2,1)} %param.11), kind=kOutput, calls=%fused_computation.1 | convolution fusion | flops 4195942400 | bytes 9830400 | tf_op jit(solution)/shard_map/dot_general | solution.py:337
  34.5 0.4 reshape.32
  34.9 1.3 copy.15
  36.2 1.9 %pad.13 = bf16[4,2,8,24,10]{4,3,2,0,1:T(8,128)(2,1)} pad(bf16[4,2,8,20,10]{4,3,2,0,1:T(8,128)(2,1)} %copy.15, bf16[]{:T(256)} %constant.51.clone.1), padding=0_0x0_0x0_0x0_4x0_0 | pad | bytes 56322 | tf_op jit(solution)/shard_map/jit(_pad)/pad | solution.py:355
  38.1 0.0 copy-done.5
  38.1 0.2 dynamic-slice_reduce_fusion.lengths_ref
  38.2 0.0 copy-done.4
  38.3 0.4 all-to-all-done
  38.7 0.9 broadcast_in_dim.13
  39.6 0.9 broadcast_in_dim.14
  40.5 8.3 %all-to-all-start.1 = ((bf16[8,160,256]{2,1,0:T(8,128)(2,1)}), bf16[8,160,256]{2,1,0:T(8,128)(2,1)}, u32[]{:S(2)}, u32[]{:S(2)}) async-start(bf16[8,160,256]{2,1,0:T(8,128)(2,1)} %broadcast_in_dim.14), calls=%async_computation.1 | async-start | bytes 1310720 | tf_op jit(solution)/shard_map/all_to_all | solution.py:312
  48.8 8.1 %fusion.vt_ref = bf16[1280,1280]{1,0:T(8,128)(2,1)} fusion(bf16[1280,1280]{1,0:T(8,128)(2,1)S(1)} %bitcast.22, bf16[1280,2560]{1,0:T(8,128)(2,1)} %param.11), kind=kOutput, calls=%fused_computation.2 | convolution fusion | flops 4195942400 | bytes 9830400 | tf_op jit(solution)/shard_map/dot_general | solution.py:339
  56.9 2.7 %all-to-all-done.1.gathered_ref = bf16[8,160,256]{2,1,0:T(8,128)(2,1)} async-done(((bf16[8,160,256]{2,1,0:T(8,128)(2,1)}), bf16[8,160,256]{2,1,0:T(8,128)(2,1)}, u32[]{:S(2)}, u32[]{:S(2)}) %all-to-all-start.1) | async-done | bytes 655392 | tf_op jit(solution)/shard_map/all_to_all | solution.py:312
  59.6 10.3 %attend.1 = bf16[8,176,256]{2,1,0:T(8,128)(2,1)S(1)} custom-call(s32[2]{0:T(128)S(1)} %dynamic-slice_reduce_fusion.lengths_ref, f32[20]{0:T(128)S(1)} %copy-done.2, bf16[8,160,256]{2,1,0:T(8,128)(2,1)} %all-to-all-done.1.gathered_ref, bf16[1280,1280]{1,0:T(8,128)(2,1)} %convolution_convert_fusion.1.k_ref, bf16[1280,1280]{1,0:T(8,128)(2,1)} %fusion.vt_ref, ...), custom_call_target="tpu_custom_call" | custom-call | tf_op jit(solution)/shard_map/attend/pallas_call | solution.py:197
  70.0 0.0 copy-start.1
  70.0 15.1 %all_to_all.30.in_ref = bf16[8,176,256]{2,1,0:T(8,128)(2,1)S(1)} all-to-all(bf16[8,176,256]{2,1,0:T(8,128)(2,1)S(1)} %attend.1), channel_id=1, replica_groups=mesh['grp'=2,'seq_0'=16,'seq_1'=4,'seq_2'=2] {'seq_1','seq_2'}, dimensions={0} | all-to-all | bytes 1441792 | tf_op jit(solution)/shard_map/all_to_all | solution.py:363
  85.1 0.3 merge.1
  85.4 20.1 %all_to_all.31.in_ref = bf16[16,32,128]{2,1,0:T(8,128)(2,1)S(1)} all-to-all(bf16[16,32,128]{2,1,0:T(8,128)(2,1)S(1)} %merge.1), channel_id=1, replica_groups=mesh['grp'=2,'seq_0'=16,'seq_1'=4,'seq_2'=2] {'seq_0'}, dimensions={0} | all-to-all | bytes 262144 | tf_op jit(solution)/shard_map/all_to_all | solution.py:371
  105.5 0.1 finish.1
  105.7 17.3 %all_to_all.32 = bf16[16,24,128]{2,1,0:T(8,128)(2,1)S(1)} all-to-all(bf16[16,24,128]{2,1,0:T(8,128)(2,1)S(1)} %broadcast_in_dim.30), channel_id=1, replica_groups=mesh['grp'=2,'seq_0'=16,'seq_1'=4,'seq_2'=2] {'seq_0'}, dimensions={0} | all-to-all | bytes 196608 | tf_op jit(solution)/shard_map/all_to_all | solution.py:312
  123.0 0.1 broadcast_in_dim.32
  123.0 8.7 %all_to_all.33 = bf16[4,384,128]{2,1,0:T(8,128)(2,1)S(1)} all-to-all(bf16[4,384,128]{2,1,0:T(8,128)(2,1)S(1)} %broadcast_in_dim.32), channel_id=1, replica_groups=mesh['grp'=2,'seq_0'=16,'seq_1'=4,'seq_2'=2] {'seq_1'}, dimensions={0} | all-to-all | bytes 786432 | tf_op jit(solution)/shard_map/all_to_all | solution.py:312
  131.7 6.3 %all-gather = bf16[8,384,128]{2,1,0:T(8,128)(2,1)S(1)} all-gather(bf16[4,384,128]{2,1,0:T(8,128)(2,1)S(1)} %all_to_all.33), channel_id=2, replica_groups=mesh['grp'=2,'seq_0'=16,'seq_1'=4,'seq_2'=2] {'seq_2'}, dimensions={0}, use_global_device_ids=true | all-gather | bytes 1179648 | tf_op jit(solution)/shard_map/all_gather | solution.py:381
  138.0 0.5 project.1
  138.5 0.7 copy.17
  (9 shorter events, 0.1 us)
Async XLA Ops:
  0.0 26.8 %copy-start = (bf16[2,640,1280]{2,1,0:T(8,128)(2,1)S(1)}, bf16[2,640,1280]{2,1,0:T(8,128)(2,1)}, u32[]{:S(2)}) copy-start(bf16[2,640,1280]{2,1,0:T(8,128)(2,1)} %param.8) | copy-start | bytes 9830404
  2.2 36.4 %all-to-all-start = ((bf16[16,16,256]{2,1,0:T(8,128)(2,1)}), bf16[16,16,256]{2,1,0:T(8,128)(2,1)}, u32[]{:S(2)}, u32[]{:S(2)}) async-start(bf16[16,16,256]{2,1,0:T(8,128)(2,1)} %broadcast_in_dim.12), calls=%async_computation | async-start | bytes 262144 | tf_op jit(solution)/shard_map/all_to_all | solution.py:312
  26.8 7.7 %copy-start.3 = (bf16[1280,10]{0,1:T(8,128)(2,1)S(1)}, bf16[1280,10]{0,1:T(8,128)(2,1)}, u32[]{:S(2)}) copy-start(bf16[1280,10]{0,1:T(8,128)(2,1)} %param.12) | copy-start | bytes 76804
  26.8 11.3 %copy-start.5 = (s32[2,128]{1,0:T(2,128)S(1)}, s32[2,128]{1,0:T(2,128)}, u32[]{:S(2)}) copy-start(s32[2,128]{1,0:T(2,128)} %param.14) | copy-start | bytes 3076
  26.8 11.4 %copy-start.4 = (s32[2,128]{1,0:T(2,128)S(1)}, s32[2,128]{1,0:T(2,128)}, u32[]{:S(2)}) copy-start(s32[2,128]{1,0:T(2,128)} %param.15) | copy-start | bytes 3076
  40.5 19.2 %all-to-all-start.1 = ((bf16[8,160,256]{2,1,0:T(8,128)(2,1)}), bf16[8,160,256]{2,1,0:T(8,128)(2,1)}, u32[]{:S(2)}, u32[]{:S(2)}) async-start(bf16[8,160,256]{2,1,0:T(8,128)(2,1)} %broadcast_in_dim.14), calls=%async_computation.1 | async-start | bytes 1310720 | tf_op jit(solution)/shard_map/all_to_all | solution.py:312
  48.8 10.9 %copy-start.2 = (f32[20]{0:T(128)S(1)}, f32[20]{0:T(128)}, u32[]{:S(2)}) copy-start(f32[20]{0:T(128)} %slope_ref.1) | copy-start | bytes 244
  70.0 68.0 %copy-start.1 = (bf16[4,2,8,24,10]{4,3,2,0,1:T(8,128)(2,1)S(1)}, bf16[4,2,8,24,10]{4,3,2,0,1:T(8,128)(2,1)}, u32[]{:S(2)}) copy-start(bf16[4,2,8,24,10]{4,3,2,0,1:T(8,128)(2,1)} %pad.13) | copy-start | bytes 92164

commit v4 on v3

--- a/solution.py
+++ b/solution.py
@@ -60,10 +60,13 @@
 def attend_kernel(
     lengths_ref,
     slope_ref,
+    core_ref,
     gathered_ref,
     k_ref,
     vt_ref,
     dist_ref,
+    mine_ref,
+    theirs_ref,
     msg_ref,
     stat_ref,
     query_ref,
@@ -150,12 +153,13 @@
             old_sum[:head_size, half:] * old_factor
             + new_sum[side * head_size : (side + 1) * head_size, late] * new_factor
         )
-        context = jnp.concatenate([old_sum[:head_size, :half], second], axis=1).astype(BF16)
+        context = jnp.concatenate([old_sum[:head_size, :half], second], axis=1)
         for part in range(head_size // SLAB):
             slab = head * (head_size // SLAB) + part
-            chunk_slabs = (msg_ref.shape[1] - 16) // SLAB
+            chunk_slabs = (msg_ref.shape[2] - 8) // SLAB
+            chunk = slab // chunk_slabs
             place = pl.multiple_of((slab % chunk_slabs) * SLAB, SLAB)
-            msg_ref[slab // chunk_slabs, pl.ds(place, SLAB), :] = context[
+            msg_ref[(chunk + core_ref[0]) % 2, chunk // 2, pl.ds(place, SLAB), :] = context[
                 part * SLAB : (part + 1) * SLAB, :
             ]
         stat_ref[head, 0:1, :] = jnp.concatenate([old_peak[:, :half], top], axis=1)
@@ -177,22 +181,25 @@
 
     @pl.when(step == last)
     def _():
-        chunk_rows = msg_ref.shape[1] - 16
+        chunk_rows = msg_ref.shape[2] - 8
         for chunk in range(chunks):
             first = chunk * chunk_rows // head_size
-            rows = []
-            for head in range(first, first + 3):
-                rows += stat_rows(stat_ref[head, 0:1, :], stat_ref[head, 1:2, :])
+            rows = [stat_ref[head, 0:2, :] for head in range(first, first + 3)]
             rows.append(jnp.zeros_like(rows[0]))
-            msg_ref[chunk, chunk_rows:, :] = jnp.concatenate(rows, axis=0).astype(BF16)
-
-
-def attend(lengths, slope, gathered, keys, values_t, dist, frame_count, columns):
+            msg_ref[(chunk + core_ref[0]) % 2, chunk // 2, chunk_rows:, :] = jnp.concatenate(
+                rows, axis=0
+            )
+        mine_ref[...] = msg_ref[0]
+        theirs_ref[...] = msg_ref[1]
+
+
+def attend(lengths, slope, core, gathered, keys, values_t, dist, frame_count, columns):
     near, _, tokens = gathered.shape
     rows, width = keys.shape
     head_count = slope.shape[0]
     head_size = width // head_count
     step_rows = PAIRS * 2 * head_size
+    part = (near // 2, width // near + 8, tokens)
     keys, values_t = (pltpu.with_memory_space_constraint(x, pltpu.HBM) for x in (keys, values_t))
     return pl.pallas_call(
         functools.partial(
@@ -206,20 +213,53 @@
         in_specs=[
             pl.BlockSpec(memory_space=pltpu.SMEM),
             pl.BlockSpec(memory_space=pltpu.SMEM),
+            pl.BlockSpec(memory_space=pltpu.SMEM),
             pl.BlockSpec(gathered.shape, lambda p: (0, 0, 0)),
             pl.BlockSpec((rows, step_rows), lambda p: (0, p)),
             pl.BlockSpec((step_rows, rows), lambda p: (p, 0)),
             pl.BlockSpec(dist.shape, lambda p: (0, 0)),
         ],
-        out_specs=pl.BlockSpec((near, width // near + 16, tokens), lambda p: (0, 0, 0)),
-        out_shape=jax.ShapeDtypeStruct((near, width // near + 16, tokens), BF16),
+        out_specs=[pl.BlockSpec(part, lambda p: (0, 0, 0))] * 2,
+        out_shape=[jax.ShapeDtypeStruct(part, F32)] * 2,
         scratch_shapes=[
+            pltpu.VMEM((2, *part), F32),
             pltpu.VMEM((head_count, 8, tokens), F32),
             pltpu.VMEM((2, PAIRS, 2 * head_size, tokens), BF16),
         ],
         compiler_params=pltpu.CompilerParams(vmem_limit_bytes=40 << 20),
         name="attend",
-    )(lengths, slope, gathered, keys, values_t, dist)
+    )(lengths, slope, core, gathered, keys, values_t, dist)
+
+
+def slab_value(values, slab, odd):
+    even_slot, odd_slot = slab // 2, (slab + 1) // 2
+    if even_slot == odd_slot:
+        return values[even_slot]
+    return jnp.where(odd, values[odd_slot], values[even_slot])
+
+
+def join_kernel(odd_ref, mine_ref, theirs_ref, out_ref):
+    chunks, rows, tokens = mine_ref.shape
+    chunk_rows = rows - 8
+    odd = odd_ref[0] == 1
+    for chunk in range(chunks):
+        own, other, stats = [], [], []
+        for slot in range(3):
+            at = chunk_rows + 2 * slot
+            peak, total = mine_ref[chunk, at : at + 1, :], mine_ref[chunk, at + 1 : at + 2, :]
+            peak_two = theirs_ref[chunk, at : at + 1, :]
+            total_two = theirs_ref[chunk, at + 1 : at + 2, :]
+            top = jnp.maximum(peak, peak_two)
+            own.append(jnp.exp(peak - top))
+            other.append(jnp.exp(peak_two - top))
+            stats += stat_rows(top, total * own[slot] + total_two * other[slot])
+        for slab in range(chunk_rows // SLAB):
+            cut = slice(slab * SLAB, (slab + 1) * SLAB)
+            joined = mine_ref[chunk, cut, :] * slab_value(own, slab, odd)
+            joined = joined + theirs_ref[chunk, cut, :] * slab_value(other, slab, odd)
+            out_ref[chunk, cut, :] = joined.astype(BF16)
+        stats.append(jnp.zeros_like(stats[0]))
+        out_ref[chunk, chunk_rows:, :] = jnp.concatenate(stats, axis=0).astype(BF16)
 
 
 def merge_kernel(odd_ref, in_ref, out_ref):
@@ -232,75 +272,84 @@
         peak = (stats[at] + stats[at + 1]) + stats[at + 2]
         top = jnp.max(peak, axis=0, keepdims=True)
         factor = jnp.exp(peak - top)
+        total = jnp.sum(factor * (stats[at + 3] + stats[at + 4]), axis=0, keepdims=True)
+        rounded = total.astype(BF16).astype(F32)
         tops.append(top)
-        factors.append(factor)
-        totals.append(jnp.sum(factor * (stats[at + 3] + stats[at + 4]), axis=0, keepdims=True))
+        totals.append(rounded)
+        factors.append(factor * (rounded / total))
     odd = odd_ref[0] == 1
     slabs, slab_stats = [], []
     for slab in range(chunk_rows // SLAB):
-        even_slot, odd_slot = slab // 2, (slab + 1) // 2
-        pick = lambda x: x[even_slot] if even_slot == odd_slot else jnp.where(odd, x[odd_slot], x[even_slot])
-        factor = pick(factors)
-        total = None
+        factor = slab_value(factors, slab, odd)
+        merged = None
         for source in range(sources):
             part = in_ref[source, slab * SLAB : (slab + 1) * SLAB, :].astype(F32)
             part = part * factor[source : source + 1, :]
-            total = part if total is None else total + part
-        slabs.append(total)
-        slab_stats.append(stat_rows(pick(tops), pick(totals)))
+            merged = part if merged is None else merged + part
+        slabs.append(merged)
+        rows = split_rows(slab_value(tops, slab, odd), PEAK_ROWS)
+        slab_stats.append(jnp.concatenate(rows + [slab_value(totals, slab, odd)], axis=0))
     merged = jnp.concatenate(slabs, axis=0)
-    targets, out_rows, lanes = out_ref.shape
+    targets, tile, width = out_ref.shape
+    lanes = tokens // 2
     pieces = targets // 2
     piece = chunk_rows // pieces
     for target in range(targets):
         side, at = target // pieces, (target % pieces) * piece
         cut = slice(side * lanes, (side + 1) * lanes)
-        rows = slab_stats[at // SLAB] + slab_stats[(at + piece - 1) // SLAB]
-        rows = [r[:, cut] for r in rows]
-        rows.append(jnp.zeros((out_rows - piece - len(rows), lanes), F32))
-        out_ref[target] = jnp.concatenate([merged[at : at + piece, cut]] + rows, axis=0).astype(BF16)
-
-
-def finish_kernel(bound_ref, in_ref, out_ref, *, piece):
-    sources, rows, lanes = in_ref.shape
-    stats = [in_ref[:, piece + r, :].astype(F32) for r in range(2 * STAT_ROWS)]
+        tiles = [merged[at + r : at + r + tile, cut] for r in range(0, piece, tile)]
+        tiles += [slab_stats[at // SLAB][:, cut], slab_stats[(at + piece - 1) // SLAB][:, cut]]
+        out_ref[target] = jnp.concatenate(tiles, axis=1).astype(BF16)
+
+
+def finish_kernel(bound_ref, in_ref, out_ref):
+    tile, width = out_ref.shape
+    lanes = (in_ref.shape[2] - width) // 2
     factors, totals = [], []
-    for at in (0, STAT_ROWS):
-        peak = (stats[at] + stats[at + 1]) + stats[at + 2]
+    for head in range(2):
+        cut = slice(width + head * lanes, width + (head + 1) * lanes)
+        stats = in_ref[:, :, cut].astype(F32)
+        peak = (stats[:, 0:1, :] + stats[:, 1:2, :]) + stats[:, 2:3, :]
         factor = jnp.exp(peak - jnp.max(peak, axis=0, keepdims=True))
         factors.append(factor)
-        totals.append(jnp.sum(factor * (stats[at + 3] + stats[at + 4]), axis=0, keepdims=True))
-    out_rows = out_ref.shape[0]
-    row = lax.broadcasted_iota(jnp.int32, (out_rows, lanes), 0)
-    first = row < bound_ref[0]
-    total = None
-    for source in range(sources):
-        factor = jnp.where(first, factors[0][source : source + 1, :], factors[1][source : source + 1, :])
-        part = in_ref[source, :out_rows, :].astype(F32) * factor
-        total = part if total is None else total + part
-    context = total / jnp.where(first, totals[0], totals[1])
-    out_ref[...] = jnp.where(row < piece, context, 0.0).astype(BF16)
-
-
-def project_kernel(ctx_ref, w_ref, out_ref):
-    pieces, sides = ctx_ref.shape[:2]
+        totals.append(jnp.sum(factor * stats[:, 3:4, :], axis=0))
+    for at in range(width // lanes):
+        cut = slice(at * lanes, (at + 1) * lanes)
+        first = at * tile < bound_ref[0]
+        factor = jnp.where(first, factors[0], factors[1])
+        context = jnp.sum(in_ref[:, :, cut].astype(F32) * factor, axis=0)
+        out_ref[:, cut] = (context / jnp.where(first, totals[0], totals[1])).astype(BF16)
+
+
+def project_kernel(ctx_ref, w_ref, out_ref, rows_ref):
+    cores, beside, targets, tile, width = ctx_ref.shape
+    sides, _, lanes = rows_ref.shape
+    pieces = targets // sides
+    piece = width // lanes * tile
+    for core in range(cores):
+        for column in range(beside):
+            chunk = column * cores + core
+            for target in range(targets):
+                held = ctx_ref[core, column, target].astype(F32)
+                top = (chunk * pieces + target % pieces) * piece
+                for at in range(width // lanes):
+                    start = top + at * tile
+                    rows_ref[target // pieces, start : start + tile, :] = held[
+                        :, at * lanes : (at + 1) * lanes
+                    ]
     for side in range(sides):
-        total = None
-        for at in range(pieces):
-            part = lax.dot_general(
-                ctx_ref[at, side], w_ref[at], (((0,), (0,)), ((), ())), preferred_element_type=F32
-            )
-            total = part if total is None else total + part
-        out_ref[side] = total.astype(BF16)
-
-
-def whole(kernel, out_shape, scalars, arrays, name):
+        out = jnp.dot(w_ref[...], rows_ref[side].astype(BF16), preferred_element_type=F32)
+        out_ref[:, side, :] = out.astype(BF16)
+
+
+def whole(kernel, out_shape, scalars, arrays, name, scratch=()):
     return pl.pallas_call(
         kernel,
         in_specs=[pl.BlockSpec(memory_space=pltpu.SMEM)] * len(scalars)
         + [pl.BlockSpec(memory_space=pltpu.VMEM)] * len(arrays),
         out_specs=pl.BlockSpec(memory_space=pltpu.VMEM),
         out_shape=out_shape,
+        scratch_shapes=scratch,
         compiler_params=pltpu.CompilerParams(vmem_limit_bytes=32 << 20),
         name=name,
     )(*scalars, *arrays)
@@ -351,42 +400,50 @@
     piece = 2 * width // devices
     at = (lax.axis_index("seq_0") % (across // 2)) * piece
     bound = (SLAB - at % SLAB).astype(jnp.int32).reshape(1)
-    weights = w_output.reshape(beside, cores, across // 2, piece, columns)
-    weights = jnp.pad(weights, ((0, 0), (0, 0), (0, 0), (0, 24 - piece), (0, 0)))
-    weights = weights.transpose(1, 0, 2, 3, 4).reshape(near, across // 2 * 24, columns)
-    queries, weights, odd, bound, dist, own_lengths = lax.optimization_barrier(
-        (queries, weights, odd, bound, dist, own_lengths)
-    )
-    message = attend(
-        own_lengths, head_slope, queries, keys, values_t, dist, frame_count, columns
-    )
-    message = lax.all_to_all(message, ("seq_1", "seq_2"), 0, 0)
+    core = lax.axis_index("seq_2").astype(jnp.int32).reshape(1)
+    queries, odd, bound, core, dist, own_lengths = lax.optimization_barrier(
+        (queries, odd, bound, core, dist, own_lengths)
+    )
+    mine, theirs = attend(
+        own_lengths, head_slope, core, queries, keys, values_t, dist, frame_count, columns
+    )
+    theirs = lax.ppermute(theirs, "seq_2", [(at, cores - 1 - at) for at in range(cores)])
+    message = whole(
+        join_kernel,
+        jax.ShapeDtypeStruct((beside, width // near + 16, tokens), BF16),
+        [odd],
+        [mine, theirs],
+        "join",
+    )
+    message = lax.all_to_all(message, "seq_1", 0, 0)
+    lanes = tokens // 2
+    tile = 4
     message = whole(
         merge_kernel,
-        jax.ShapeDtypeStruct((across, SLAB, tokens // 2), BF16),
+        jax.ShapeDtypeStruct((across, tile, (piece // tile + 2) * lanes), BF16),
         [odd],
         [message],
         "merge",
     )
     message = lax.all_to_all(message, "seq_0", 0, 0)
     context = whole(
-        functools.partial(finish_kernel, piece=piece),
-        jax.ShapeDtypeStruct((24, tokens // 2), BF16),
+        finish_kernel,
+        jax.ShapeDtypeStruct((tile, piece // tile * lanes), BF16),
         [bound],
         [message],
         "finish",
     )
-    context = spread(context, "seq_0")
-    context = spread(context.reshape(across * 24, tokens // 2), "seq_1")
+    context = spread(spread(context, "seq_0"), "seq_1")
     context = lax.all_gather(context, "seq_2")
-    context = context.reshape(near, 2, across // 2 * 24, tokens // 2)
-    return whole(
+    out = whole(
         project_kernel,
-        jax.ShapeDtypeStruct((step_count, query_rows, columns), BF16),
+        jax.ShapeDtypeStruct((columns, step_count, query_rows), BF16),
         [],
-        [context, weights],
+        [context, w_output.T],
         "project",
-    )
+        [pltpu.VMEM((2, width, lanes), F32)],
+    )
+    return out.transpose(1, 2, 0)
 
 
 def solution(mesh):

time: 140 us -> 132 us (0.943)
  blocking collectives: 67.5 us -> 57.4 us
  waiting for transfers between devices: 3.12 us -> 8.36 us
  local copies, waits for them, and re-layouts: 7.06 us -> 2.2 us
    all_to_all x1, blocking collectives: 15.1 us -> 9.86 us  [local(): message = lax.all_to_all(message, 'seq_1', 0, 0)]
    all_to_all x1, blocking collectives: 20.1 us -> 16.6 us  [local(): message = lax.all_to_all(message, 'seq_0', 0, 0)]
    all_to_all x2, waiting for transfers between devices: 3.12 us -> 6.59 us  [spread(): return lax.all_to_all(copies, axis, 0, 0)]
    pad x1 -> x0, local copies, waits for them, and re-layouts: 1.87 us -> none  [local(): jnp.pad(weights, ((0, 0), (0, 0), (0, 0), (0, 24 - piece), (0, 0)))]
    ppermute x0 -> x1, waiting for transfers between devices: none -> 1.77 us  [local(): lax.ppermute(theirs, 'seq_2', [(at, cores - 1 - at) for at in range(cores)])]
    reshape x2 -> x0, local copies, waits for them, and re-layouts: 1.67 us -> none  [local(): weights = w_output.reshape(beside, cores, across // 2, piece, columns)]
  transfers between devices with their start and end apart: 2 -> 3, of which waited for: 2 -> 3; matrix products, arithmetic and copies ran while one was open for 14% -> 12% of each run, Pallas kernels for 0% -> 0%
where the time goes in v4:
time: 132 us; the launch traced here: 131 us
  blocking collectives  57.4 us (43%)
  starting transfers between devices  33.9 us (26%)
  matrix products  17.3 us (13%)
  Pallas kernels  11.9 us (9%)
  waiting for transfers between devices  8.36 us (6%)
  local copies, waits for them, and re-layouts  2.2 us (2%)
    all_to_all x2, starting transfers between devices, spread(): return lax.all_to_all(copies, axis, 0, 0)  32.8 us
    all_to_all x2, blocking collectives, spread(): return lax.all_to_all(copies, axis, 0, 0)  24.9 us
    all_to_all x1, blocking collectives, local(): message = lax.all_to_all(message, 'seq_0', 0, 0)  16.6 us
    pallas_call x1, Pallas kernels, attend(): pl.pallas_call(functools.partial(attend_kernel, frame_count=frame_count,...  10.4 us
    all_to_all x1, blocking collectives, local(): message = lax.all_to_all(message, 'seq_1', 0, 0)  9.86 us
    dot_general x1, matrix products, local(): lax.dot_general(w_keyval[:, width:], late_rows, (((0,), (1,)), ((), ())),...  8.11 us
    dot_general x1, matrix products, local(): jnp.dot(frame_rows, w_keyval[:, :width], preferred_element_type=F32)  7.68 us
    all_to_all x2, waiting for transfers between devices, spread(): return lax.all_to_all(copies, axis, 0, 0)  6.59 us
  transfers between devices with their start and end apart: 3, of which 3 were waited for; matrix products, arithmetic and copies ran while one was open for 12% of the time, Pallas kernels for 0%

profile of v4, /device:TPU:33, one launch (start us, length us, event | category | flops | bytes accessed | tf_op | source)
XLA Modules:
  0.0 131.2 jit_solution(281184679305716933)
XLA Ops:
  0.0 0.0 copy-start
  0.0 1.5 %convolution_convert_fusion.2 = bf16[10,256]{1,0:T(8,128)(2,1)S(1)} fusion(bf16[1280,10]{0,1:T(8,128)(2,1)} %param.10, bf16[256,1280]{1,0:T(8,128)(2,1)} %bitcast.22), kind=kOutput, calls=%fused_computation.5 | convolution fusion | flops 6556160 | bytes 686080 | tf_op jit(solution)/shard_map/dot_general | solution.py:374
  1.5 0.1 pad.8
  1.6 0.7 broadcast_in_dim.10
  2.3 24.5 %all-to-all-start = ((bf16[16,16,256]{2,1,0:T(8,128)(2,1)}), bf16[16,16,256]{2,1,0:T(8,128)(2,1)S(1)}, u32[]{:S(2)}, u32[]{:S(2)}) async-start(bf16[16,16,256]{2,1,0:T(8,128)(2,1)} %broadcast_in_dim.10), calls=%async_computation | async-start | bytes 262144 | tf_op jit(solution)/shard_map/all_to_all | solution.py:361
  26.8 0.0 copy-done
  26.8 0.0 copy-start.4
  26.8 0.0 copy-start.3
  26.8 7.7 %convolution_convert_fusion.1.k_ref = bf16[1280,1280]{1,0:T(8,128)(2,1)} fusion(bf16[1280,1280]{1,0:T(8,128)(2,1)S(1)} %bitcast.18, bf16[1280,2560]{1,0:T(8,128)(2,1)} %param.11), kind=kOutput, calls=%fused_computation.1 | convolution fusion | flops 4195942400 | bytes 9830400 | tf_op jit(solution)/shard_map/dot_general | solution.py:386
  34.5 0.0 copy-done.4
  34.5 0.2 dynamic-slice_reduce_fusion.lengths_ref
  34.7 0.0 copy-done.3
  34.7 3.8 %all-to-all-done = bf16[16,16,256]{2,1,0:T(8,128)(2,1)S(1)} async-done(((bf16[16,16,256]{2,1,0:T(8,128)(2,1)}), bf16[16,16,256]{2,1,0:T(8,128)(2,1)S(1)}, u32[]{:S(2)}, u32[]{:S(2)}) %all-to-all-start) | async-done | bytes 131104 | tf_op jit(solution)/shard_map/all_to_all | solution.py:361
  38.6 0.9 broadcast_in_dim.12
  39.5 8.3 %all-to-all-start.1 = ((bf16[8,160,256]{2,1,0:T(8,128)(2,1)}), bf16[8,160,256]{2,1,0:T(8,128)(2,1)}, u32[]{:S(2)}, u32[]{:S(2)}) async-start(bf16[8,160,256]{2,1,0:T(8,128)(2,1)} %broadcast_in_dim.12), calls=%async_computation.1 | async-start | bytes 1310720 | tf_op jit(solution)/shard_map/all_to_all | solution.py:361
  47.8 8.1 %fusion.vt_ref = bf16[1280,1280]{1,0:T(8,128)(2,1)} fusion(bf16[1280,1280]{1,0:T(8,128)(2,1)S(1)} %bitcast.19, bf16[1280,2560]{1,0:T(8,128)(2,1)} %param.11), kind=kOutput, calls=%fused_computation.2 | convolution fusion | flops 4195942400 | bytes 9830400 | tf_op jit(solution)/shard_map/dot_general | solution.py:388
  55.9 2.7 %all-to-all-done.1.gathered_ref = bf16[8,160,256]{2,1,0:T(8,128)(2,1)} async-done(((bf16[8,160,256]{2,1,0:T(8,128)(2,1)}), bf16[8,160,256]{2,1,0:T(8,128)(2,1)}, u32[]{:S(2)}, u32[]{:S(2)}) %all-to-all-start.1) | async-done | bytes 655392 | tf_op jit(solution)/shard_map/all_to_all | solution.py:361
  58.6 0.0 copy-done.2
  58.6 10.4 %attend.1 = (f32[4,168,256]{2,1,0:T(8,128)S(1)}, f32[4,168,256]{2,1,0:T(8,128)S(1)}) custom-call(s32[2]{0:T(128)S(1)} %dynamic-slice_reduce_fusion.lengths_ref, f32[20]{0:T(128)S(1)} %copy-done.2, s32[1]{0:T(128)} %bitcast.3.core_ref, bf16[8,160,256]{2,1,0:T(8,128)(2,1)} %all-to-all-done.1.gathered_ref, bf16[1280,1280]{1,0:T(8,128)(2,1)} %convolution_convert_fusion.1.k_ref, ...), custom_call_target="tpu_custom_call" | custom-call | tf_op jit(solution)/shard_map/attend/pallas_call | solution.py:204
  69.1 1.1 collective-permute-start
  70.2 1.8 %collective-permute-done.theirs_ref = f32[4,168,256]{2,1,0:T(8,128)S(1)} collective-permute-done((f32[4,168,256]{2,1,0:T(8,128)S(1)}, f32[4,168,256]{2,1,0:T(8,128)S(1)}, u32[]{:S(2)}, u32[]{:S(2)}) %collective-permute-start) | collective-permute-done | bytes 688160 | tf_op jit(solution)/shard_map/ppermute | solution.py:410
  72.0 0.2 join.1
  72.2 9.9 %all_to_all.30.in_ref = bf16[4,176,256]{2,1,0:T(8,128)(2,1)S(1)} all-to-all(bf16[4,176,256]{2,1,0:T(8,128)(2,1)S(1)} %join.1), channel_id=1, replica_groups=mesh['grp'=2,'seq_0'=16,'seq_1'=4,'seq_2'=2] {'seq_1'}, dimensions={0} | all-to-all | bytes 720896 | tf_op jit(solution)/shard_map/all_to_all | solution.py:418
  82.0 0.2 merge.1
  82.2 16.6 %all_to_all.31.in_ref = bf16[16,4,896]{2,1,0:T(4,128)(2,1)S(1)} all-to-all(bf16[16,4,896]{2,1,0:T(4,128)(2,1)S(1)} %merge.1), channel_id=1, replica_groups=mesh['grp'=2,'seq_0'=16,'seq_1'=4,'seq_2'=2] {'seq_0'}, dimensions={0} | all-to-all | bytes 229376 | tf_op jit(solution)/shard_map/all_to_all | solution.py:428
  98.8 0.1 finish.1
  99.0 16.6 %all_to_all.32 = bf16[16,4,640]{2,1,0:T(4,128)(2,1)S(1)} all-to-all(bf16[16,4,640]{2,1,0:T(4,128)(2,1)S(1)} %broadcast_in_dim.13), channel_id=1, replica_groups=mesh['grp'=2,'seq_0'=16,'seq_1'=4,'seq_2'=2] {'seq_0'}, dimensions={0} | all-to-all | bytes 163840 | tf_op jit(solution)/shard_map/all_to_all | solution.py:361
  115.6 8.3 %all_to_all.33 = bf16[4,16,4,640]{3,1,2,0:T(8,128)(2,1)S(1)} all-to-all(bf16[4,16,4,640]{3,1,2,0:T(8,128)(2,1)S(1)} %broadcast_in_dim.14), channel_id=1, replica_groups=mesh['grp'=2,'seq_0'=16,'seq_1'=4,'seq_2'=2] {'seq_1'}, dimensions={0} | all-to-all | bytes 655360 | tf_op jit(solution)/shard_map/all_to_all | solution.py:361
  123.9 6.1 %all-gather = bf16[8,16,4,640]{3,1,2,0:T(8,128)(2,1)S(1)} all-gather(bf16[4,16,4,640]{3,1,2,0:T(8,128)(2,1)S(1)} %all_to_all.33), channel_id=2, replica_groups=mesh['grp'=2,'seq_0'=16,'seq_1'=4,'seq_2'=2] {'seq_2'}, dimensions={0}, use_global_device_ids=true | all-gather | bytes 983040 | tf_op jit(solution)/shard_map/all_gather | solution.py:437
  130.0 0.3 copy.15
  130.3 0.0 copy-done.1
  130.3 0.9 project.1
  (8 shorter events, 0.1 us)
Async XLA Ops:
  0.0 26.8 %copy-start = (bf16[2,640,1280]{2,1,0:T(8,128)(2,1)S(1)}, bf16[2,640,1280]{2,1,0:T(8,128)(2,1)}, u32[]{:S(2)}) copy-start(bf16[2,640,1280]{2,1,0:T(8,128)(2,1)} %param.8) | copy-start | bytes 9830404
  2.3 36.3 %all-to-all-start = ((bf16[16,16,256]{2,1,0:T(8,128)(2,1)}), bf16[16,16,256]{2,1,0:T(8,128)(2,1)S(1)}, u32[]{:S(2)}, u32[]{:S(2)}) async-start(bf16[16,16,256]{2,1,0:T(8,128)(2,1)} %broadcast_in_dim.10), calls=%async_computation | async-start | bytes 262144 | tf_op jit(solution)/shard_map/all_to_all | solution.py:361
  26.8 7.7 %copy-start.4 = (s32[2,128]{1,0:T(2,128)S(1)}, s32[2,128]{1,0:T(2,128)}, u32[]{:S(2)}) copy-start(s32[2,128]{1,0:T(2,128)} %param.14) | copy-start | bytes 3076
  26.8 7.9 %copy-start.3 = (s32[2,128]{1,0:T(2,128)S(1)}, s32[2,128]{1,0:T(2,128)}, u32[]{:S(2)}) copy-start(s32[2,128]{1,0:T(2,128)} %param.15) | copy-start | bytes 3076
  39.5 19.2 %all-to-all-start.1 = ((bf16[8,160,256]{2,1,0:T(8,128)(2,1)}), bf16[8,160,256]{2,1,0:T(8,128)(2,1)}, u32[]{:S(2)}, u32[]{:S(2)}) async-start(bf16[8,160,256]{2,1,0:T(8,128)(2,1)} %broadcast_in_dim.12), calls=%async_computation.1 | async-start | bytes 1310720 | tf_op jit(solution)/shard_map/all_to_all | solution.py:361
  47.8 10.9 %copy-start.2 = (f32[20]{0:T(128)S(1)}, f32[20]{0:T(128)}, u32[]{:S(2)}) copy-start(f32[20]{0:T(128)} %slope_ref.1) | copy-start | bytes 244
  69.1 2.9 %collective-permute-start = (f32[4,168,256]{2,1,0:T(8,128)S(1)}, f32[4,168,256]{2,1,0:T(8,128)S(1)}, u32[]{:S(2)}, u32[]{:S(2)}) collective-permute-start(f32[4,168,256]{2,1,0:T(8,128)S(1)} %get-tuple-element.24), channel_id=1, source_target_pairs={{0,1},{1,0},{2,3},{3,2},{4,5},{5,4},{6,7},{7,6},{8,9},{9,8},{10,11... | collective-permute-start | bytes 2064392 | tf_op jit(solution)/shard_map/ppermute | solution.py:410
  72.0 58.3 %copy-start.1 = (bf16[1280,10]{0,1:T(8,128)(2,1)S(1)}, bf16[1280,10]{0,1:T(8,128)(2,1)}, u32[]{:S(2)}) copy-start(bf16[1280,10]{0,1:T(8,128)(2,1)} %param.12) | copy-start | bytes 76804

commit v5 on v4

--- a/solution.py
+++ b/solution.py
@@ -39,6 +39,7 @@
 
 def pair_queries(pair, gathered_ref, rows, columns):
     near, held, _ = gathered_ref.shape
+    held -= 16
     window = 48
     span = near * columns
     first = jnp.minimum((pair * rows // span) * columns // 16, (held - window) // 16)
@@ -321,25 +322,78 @@
         out_ref[:, cut] = (context / jnp.where(first, totals[0], totals[1])).astype(BF16)
 
 
+def ask_kernel(w_ref, dec_ref, out_ref):
+    columns, tokens = w_ref.shape[0], dec_ref.shape[0]
+    lanes = tokens // 2
+    queries = lax.dot_general(
+        w_ref[...], dec_ref[...], (((1,), (1,)), ((), ())), preferred_element_type=F32
+    )
+    sides = [queries[:, :lanes], queries[:, lanes:]]
+    tiles = [side[at : at + 4] for side in sides for at in range(0, columns - 2, 4)]
+    tiles.append(jnp.concatenate([side[columns - 2 :] for side in sides], axis=0))
+    tiles = jnp.concatenate(tiles, axis=1).astype(BF16)
+    for target in range(out_ref.shape[0]):
+        out_ref[target] = tiles
+
+
+def columns_kernel(w_ref, out_ref):
+    chunks, rows, lanes = out_ref.shape
+    columns, width = w_ref.shape
+    part = width // chunks
+    weights = w_ref[...].astype(F32)
+    for chunk in range(chunks):
+        own = weights[:, chunk * part : (chunk + 1) * part]
+        own = jnp.concatenate([own, jnp.zeros((columns, lanes - part), F32)], axis=1)
+        own = jnp.concatenate([own, jnp.zeros((rows - columns, lanes), F32)], axis=0)
+        out_ref[chunk] = own.astype(BF16)
+
+
+def pack_kernel(tiles_ref, w_ref, out_ref, rows_ref, *, columns):
+    targets = tiles_ref.shape[0]
+    tokens = out_ref.shape[2]
+    lanes = tokens // 2
+    whole_tiles = (columns - 2) // 4
+    for source in range(targets):
+        held = tiles_ref[source].astype(F32)
+        tiles = [held[:, at * lanes : (at + 1) * lanes] for at in range(2 * whole_tiles + 1)]
+        top = source * columns
+        for side in range(2):
+            cut = slice(side * lanes, (side + 1) * lanes)
+            for at in range(whole_tiles):
+                rows_ref[top + 4 * at : top + 4 * at + 4, cut] = tiles[side * whole_tiles + at]
+            rows_ref[top + columns - 2 : top + columns, cut] = tiles[-1][2 * side : 2 * side + 2]
+    rows = rows_ref[...].astype(BF16)
+    for target in range(out_ref.shape[0]):
+        out_ref[target, : rows.shape[0], :] = rows
+        out_ref[target, rows.shape[0] :, :] = w_ref[target]
+
+
 def project_kernel(ctx_ref, w_ref, out_ref, rows_ref):
-    cores, beside, targets, tile, width = ctx_ref.shape
-    sides, _, lanes = rows_ref.shape
-    pieces = targets // sides
+    targets, tile, width = ctx_ref.shape
+    part, tokens = rows_ref.shape
+    lanes = tokens // 2
+    pieces = targets // 2
     piece = width // lanes * tile
-    for core in range(cores):
-        for column in range(beside):
-            chunk = column * cores + core
-            for target in range(targets):
-                held = ctx_ref[core, column, target].astype(F32)
-                top = (chunk * pieces + target % pieces) * piece
-                for at in range(width // lanes):
-                    start = top + at * tile
-                    rows_ref[target // pieces, start : start + tile, :] = held[
-                        :, at * lanes : (at + 1) * lanes
-                    ]
+    for target in range(targets):
+        held = ctx_ref[target].astype(F32)
+        side = target // pieces
+        for at in range(width // lanes):
+            start = (target % pieces) * piece + at * tile
+            rows_ref[start : start + tile, side * lanes : (side + 1) * lanes] = held[
+                :, at * lanes : (at + 1) * lanes
+            ]
+    sources, rows, _ = w_ref.shape
+    weights = jnp.concatenate([w_ref[source, :, :part] for source in range(sources)], axis=0)
+    out = jnp.dot(weights, rows_ref[...].astype(BF16), preferred_element_type=F32)
+    for source in range(sources):
+        out_ref[source] = out[source * rows : (source + 1) * rows]
+
+
+def sum_kernel(in_ref, out_ref):
+    columns, sides, lanes = out_ref.shape
+    total = jnp.sum(in_ref[...], axis=0)
     for side in range(sides):
-        out = jnp.dot(w_ref[...], rows_ref[side].astype(BF16), preferred_element_type=F32)
-        out_ref[:, side, :] = out.astype(BF16)
+        out_ref[:, side, :] = total[:columns, side * lanes : (side + 1) * lanes].astype(BF16)
 
 
 def whole(kernel, out_shape, scalars, arrays, name, scratch=()):
@@ -371,16 +425,37 @@
     columns = w_query.shape[1]
     near = beside * cores
 
-    own_queries = lax.dot_general(
-        w_query,
-        dec_states.reshape(tokens, width),
-        (((0,), (1,)), ((), ())),
-        preferred_element_type=F32,
-    ).astype(BF16)
-    padded = jnp.pad(own_queries, ((0, 16 - columns), (0, 0)))
-    queries = spread(padded, "seq_0")[:, :columns]
+    lanes = tokens // 2
+    tile = 4
+    part = width // near
+    asked = whole(
+        ask_kernel,
+        jax.ShapeDtypeStruct((across, tile, columns * tokens // tile), BF16),
+        [],
+        [
+            pltpu.with_memory_space_constraint(x, pltpu.HBM)
+            for x in (w_query.T, dec_states.reshape(tokens, width))
+        ],
+        "ask",
+    )
+    out_columns = whole(
+        columns_kernel,
+        jax.ShapeDtypeStruct((near, 16, tokens), BF16),
+        [],
+        [w_output.T],
+        "columns",
+    )
+    queries = lax.all_to_all(asked, "seq_0", 0, 0)
     queries, late_frames = lax.optimization_barrier((queries, frames))
-    queries = spread(queries.reshape(across * columns, tokens), SEQ[1:])
+    queries = whole(
+        functools.partial(pack_kernel, columns=columns),
+        pltpu.HBM((near, part + 16, tokens), BF16),
+        [],
+        [queries, out_columns],
+        "pack",
+        [pltpu.VMEM((part, tokens), F32)],
+    )
+    queries = lax.all_to_all(queries, SEQ[1:], 0, 0)
 
     frame_rows = frames.reshape(step_count * frame_count, width)
     keys = jnp.dot(frame_rows, w_keyval[:, :width], preferred_element_type=F32).astype(BF16)
@@ -407,7 +482,10 @@
     mine, theirs = attend(
         own_lengths, head_slope, core, queries, keys, values_t, dist, frame_count, columns
     )
+    theirs, asked_columns = lax.optimization_barrier((theirs, queries))
+    out_columns = asked_columns[:, part:, :]
     theirs = lax.ppermute(theirs, "seq_2", [(at, cores - 1 - at) for at in range(cores)])
+    theirs, out_columns = lax.optimization_barrier((theirs, out_columns))
     message = whole(
         join_kernel,
         jax.ShapeDtypeStruct((beside, width // near + 16, tokens), BF16),
@@ -416,8 +494,6 @@
         "join",
     )
     message = lax.all_to_all(message, "seq_1", 0, 0)
-    lanes = tokens // 2
-    tile = 4
     message = whole(
         merge_kernel,
         jax.ShapeDtypeStruct((across, tile, (piece // tile + 2) * lanes), BF16),
@@ -433,15 +509,22 @@
         [message],
         "finish",
     )
-    context = spread(spread(context, "seq_0"), "seq_1")
-    context = lax.all_gather(context, "seq_2")
+    context = spread(context, "seq_0")
+    partial = whole(
+        project_kernel,
+        jax.ShapeDtypeStruct((near, 16, tokens), F32),
+        [],
+        [context, out_columns],
+        "project",
+        [pltpu.VMEM((part, tokens), F32)],
+    )
+    partial = lax.all_to_all(partial, SEQ[1:], 0, 0)
     out = whole(
-        project_kernel,
+        sum_kernel,
         jax.ShapeDtypeStruct((columns, step_count, query_rows), BF16),
         [],
-        [context, w_output.T],
-        "project",
-        [pltpu.VMEM((2, width, lanes), F32)],
+        [partial],
+        "sum",
     )
     return out.transpose(1, 2, 0)
 

time: 132 us -> 130 us (0.985)
  Pallas kernels: 11.9 us -> 15.1 us
  waiting for transfers between devices: 8.36 us -> 6.43 us
  matrix products: 17.3 us -> 15.8 us
  starting transfers between devices: 33.9 us -> 32.4 us
    all_to_all x0 -> x1, blocking collectives: none -> 10.7 us  [local(): partial = lax.all_to_all(partial, SEQ[1:], 0, 0)]
    all_to_all x2 -> x1, blocking collectives: 24.9 us -> 16.6 us  [spread(): return lax.all_to_all(copies, axis, 0, 0)]
    all_gather x1 -> x0, blocking collectives: 6.08 us -> none  [local(): context = lax.all_gather(context, 'seq_2')]
    all_to_all x1, blocking collectives: 16.6 us -> 19.8 us  [local(): message = lax.all_to_all(message, 'seq_0', 0, 0)]
    pallas_call x4 -> x8, Pallas kernels: 1.48 us -> 4.57 us  [whole(): pl.pallas_call(kernel, in_specs=[pl.BlockSpec(memory_space=pltpu.SMEM)] *...]
    broadcast_in_dim x5 -> x1, local copies, waits for them, and re-layouts: 1.64 us -> 0.03 us  [spread(): copies = jnp.broadcast_to(x[None], (lax.axis_size(axis), *x.shape))]
    dot_general x1 -> x0, matrix products: 1.5 us -> none  [local(): lax.dot_general(w_query, dec_states.reshape(tokens, width), (((0,), (1,))...]
    all_to_all x2, starting transfers between devices: 32.8 us -> 31.3 us  [the longest x1 24.5 us: local(): queries = lax.all_to_all(asked, 'seq_0', 0, 0)]
  transfers between devices with their start and end apart: 3 -> 3, of which waited for: 3 -> 3; matrix products, arithmetic and copies ran while one was open for 12% -> 14% of each run, Pallas kernels for 0% -> 0%
where the time goes in v5:
time: 130 us; the launch traced here: 129 us
  blocking collectives  56.9 us (44%)
  starting transfers between devices  32.4 us (25%)
  matrix products  15.8 us (12%)
  Pallas kernels  15.1 us (12%)
  waiting for transfers between devices  6.43 us (5%)
  local copies, waits for them, and re-layouts  2.53 us (2%)
    all_to_all x1, starting transfers between devices, local(): queries = lax.all_to_all(asked, 'seq_0', 0, 0)  24.5 us
    all_to_all x1, blocking collectives, local(): message = lax.all_to_all(message, 'seq_0', 0, 0)  19.8 us
    all_to_all x1, blocking collectives, spread(): return lax.all_to_all(copies, axis, 0, 0)  16.6 us
    all_to_all x1, blocking collectives, local(): partial = lax.all_to_all(partial, SEQ[1:], 0, 0)  10.7 us
    pallas_call x1, Pallas kernels, attend(): pl.pallas_call(functools.partial(attend_kernel, frame_count=frame_count,...  10.5 us
    all_to_all x1, blocking collectives, local(): message = lax.all_to_all(message, 'seq_1', 0, 0)  9.86 us
    dot_general x1, matrix products, local(): lax.dot_general(w_keyval[:, width:], late_rows, (((0,), (1,)), ((), ())),...  8.11 us
    dot_general x1, matrix products, local(): jnp.dot(frame_rows, w_keyval[:, :width], preferred_element_type=F32)  7.69 us
  transfers between devices with their start and end apart: 3, of which 3 were waited for; matrix products, arithmetic and copies ran while one was open for 14% of the time, Pallas kernels for 0%

profile of v5, /device:TPU:33, one launch (start us, length us, event | category | flops | bytes accessed | tf_op | source)
XLA Modules:
  0.0 129.3 jit_solution(5462417337112562813)
XLA Ops:
  0.0 0.0 copy-start
  0.0 2.2 %ask.1 = bf16[16,4,640]{2,1,0:T(4,128)(2,1)} custom-call(bf16[10,1280]{1,0:T(8,128)(2,1)} %bitcast.19, bf16[256,1280]{1,0:T(8,128)(2,1)} %bitcast.18), custom_call_target="tpu_custom_call" | custom-call | tf_op jit(solution)/shard_map/ask/pallas_call | solution.py:400
  2.2 24.5 %all-to-all-start = ((bf16[16,4,640]{2,1,0:T(4,128)(2,1)}), bf16[16,4,640]{2,1,0:T(4,128)(2,1)S(1)}, u32[]{:S(2)}, u32[]{:S(2)}) async-start(bf16[16,4,640]{2,1,0:T(4,128)(2,1)} %ask.1), calls=%async_computation | async-start | bytes 163840 | tf_op jit(solution)/shard_map/all_to_all | solution.py:448
  26.8 0.0 copy-start.1
  26.8 0.8 copy-done.1
  27.6 0.1 columns.1.w_ref
  27.7 0.9 dynamic-slice_reduce_fusion.lengths_ref
  28.5 0.0 copy-done
  28.5 0.0 copy-start.3
  28.6 7.7 %convolution_convert_fusion.1.k_ref = bf16[1280,1280]{1,0:T(8,128)(2,1)} fusion(bf16[1280,1280]{1,0:T(8,128)(2,1)S(1)} %bitcast.15, bf16[1280,2560]{1,0:T(8,128)(2,1)} %param.11), kind=kOutput, calls=%fused_computation.1 | convolution fusion | flops 4195942400 | bytes 9830400 | tf_op jit(solution)/shard_map/dot_general | solution.py:461
  36.2 0.0 copy-done.3
  36.3 2.1 %all-to-all-done.tiles_ref = bf16[16,4,640]{2,1,0:T(4,128)(2,1)S(1)} async-done(((bf16[16,4,640]{2,1,0:T(4,128)(2,1)}), bf16[16,4,640]{2,1,0:T(4,128)(2,1)S(1)}, u32[]{:S(2)}, u32[]{:S(2)}) %all-to-all-start) | async-done | bytes 81952 | tf_op jit(solution)/shard_map/all_to_all | solution.py:448
  38.3 0.9 pack.1
  39.3 6.8 %all-to-all-start.1 = ((bf16[8,176,256]{2,1,0:T(8,128)(2,1)}), bf16[8,176,256]{2,1,0:T(8,128)(2,1)}, u32[]{:S(2)}, u32[]{:S(2)}) async-start(bf16[8,176,256]{2,1,0:T(8,128)(2,1)} %pack.1), calls=%async_computation.1 | async-start | bytes 1441792 | tf_op jit(solution)/shard_map/all_to_all | solution.py:458
  46.1 0.0 copy-start.2
  46.1 8.1 %fusion.vt_ref = bf16[1280,1280]{1,0:T(8,128)(2,1)} fusion(bf16[1280,1280]{1,0:T(8,128)(2,1)S(1)} %bitcast.16, bf16[1280,2560]{1,0:T(8,128)(2,1)} %param.11), kind=kOutput, calls=%fused_computation.2 | convolution fusion | flops 4195942400 | bytes 9830400 | tf_op jit(solution)/shard_map/dot_general | solution.py:463
  54.2 3.4 %all-to-all-done.1.gathered_ref = bf16[8,176,256]{2,1,0:T(8,128)(2,1)} async-done(((bf16[8,176,256]{2,1,0:T(8,128)(2,1)}), bf16[8,176,256]{2,1,0:T(8,128)(2,1)}, u32[]{:S(2)}, u32[]{:S(2)}) %all-to-all-start.1) | async-done | bytes 720928 | tf_op jit(solution)/shard_map/all_to_all | solution.py:458
  57.7 0.0 copy-done.2
  57.7 10.5 %attend.1 = (f32[4,168,256]{2,1,0:T(8,128)S(1)}, f32[4,168,256]{2,1,0:T(8,128)S(1)}) custom-call(s32[2]{0:T(128)S(1)} %dynamic-slice_reduce_fusion.lengths_ref, f32[20]{0:T(128)S(1)} %copy-done.2, s32[1]{0:T(128)} %bitcast.5.core_ref, bf16[8,176,256]{2,1,0:T(8,128)(2,1)} %all-to-all-done.1.gathered_ref, bf16[1280,1280]{1,0:T(8,128)(2,1)} %convolution_convert_fusion.1.k_ref, ...), custom_call_target="tpu_custom_call" | custom-call | tf_op jit(solution)/shard_map/attend/pallas_call | solution.py:205
  68.1 1.1 collective-permute-start
  69.2 0.8 slice.11.w_ref
  70.1 0.9 collective-permute-done.theirs_ref
  71.0 0.2 join.1
  71.2 9.9 %all_to_all.30.in_ref = bf16[4,176,256]{2,1,0:T(8,128)(2,1)S(1)} all-to-all(bf16[4,176,256]{2,1,0:T(8,128)(2,1)S(1)} %join.1), channel_id=1, replica_groups=mesh['grp'=2,'seq_0'=16,'seq_1'=4,'seq_2'=2] {'seq_1'}, dimensions={0} | all-to-all | bytes 720896 | tf_op jit(solution)/shard_map/all_to_all | solution.py:496
  81.1 0.2 merge.1
  81.3 19.8 %all_to_all.31.in_ref = bf16[16,4,896]{2,1,0:T(4,128)(2,1)S(1)} all-to-all(bf16[16,4,896]{2,1,0:T(4,128)(2,1)S(1)} %merge.1), channel_id=1, replica_groups=mesh['grp'=2,'seq_0'=16,'seq_1'=4,'seq_2'=2] {'seq_0'}, dimensions={0} | all-to-all | bytes 229376 | tf_op jit(solution)/shard_map/all_to_all | solution.py:504
  101.1 0.1 finish.1
  101.2 16.6 %all_to_all.32.ctx_ref = bf16[16,4,640]{2,1,0:T(4,128)(2,1)S(1)} all-to-all(bf16[16,4,640]{2,1,0:T(4,128)(2,1)S(1)} %broadcast_in_dim.2), channel_id=1, replica_groups=mesh['grp'=2,'seq_0'=16,'seq_1'=4,'seq_2'=2] {'seq_0'}, dimensions={0} | all-to-all | bytes 163840 | tf_op jit(solution)/shard_map/all_to_all | solution.py:415
  117.8 0.2 project.1
  118.0 10.7 %all_to_all.33.in_ref = f32[8,16,256]{2,1,0:T(8,128)S(1)} all-to-all(f32[8,16,256]{2,1,0:T(8,128)S(1)} %project.1), channel_id=1, replica_groups=mesh['grp'=2,'seq_0'=16,'seq_1'=4,'seq_2'=2] {'seq_1','seq_2'}, dimensions={0} | all-to-all | bytes 262144 | tf_op jit(solution)/shard_map/all_to_all | solution.py:521
  128.7 0.6 sum.1
  (3 shorter events, 0.0 us)
Async XLA Ops:
  0.0 28.5 %copy-start = (bf16[2,640,1280]{2,1,0:T(8,128)(2,1)S(1)}, bf16[2,640,1280]{2,1,0:T(8,128)(2,1)}, u32[]{:S(2)}) copy-start(bf16[2,640,1280]{2,1,0:T(8,128)(2,1)} %param.8) | copy-start | bytes 9830404
  2.2 36.1 %all-to-all-start = ((bf16[16,4,640]{2,1,0:T(4,128)(2,1)}), bf16[16,4,640]{2,1,0:T(4,128)(2,1)S(1)}, u32[]{:S(2)}, u32[]{:S(2)}) async-start(bf16[16,4,640]{2,1,0:T(4,128)(2,1)} %ask.1), calls=%async_computation | async-start | bytes 163840 | tf_op jit(solution)/shard_map/all_to_all | solution.py:448
  26.8 0.8 copy-start.1
  28.5 7.7 %copy-start.3 = (s32[2,128]{1,0:T(2,128)S(1)}, s32[2,128]{1,0:T(2,128)}, u32[]{:S(2)}) copy-start(s32[2,128]{1,0:T(2,128)} %param.15) | copy-start | bytes 3076
  39.3 18.4 %all-to-all-start.1 = ((bf16[8,176,256]{2,1,0:T(8,128)(2,1)}), bf16[8,176,256]{2,1,0:T(8,128)(2,1)}, u32[]{:S(2)}, u32[]{:S(2)}) async-start(bf16[8,176,256]{2,1,0:T(8,128)(2,1)} %pack.1), calls=%async_computation.1 | async-start | bytes 1441792 | tf_op jit(solution)/shard_map/all_to_all | solution.py:458
  46.1 11.6 %copy-start.2 = (f32[20]{0:T(128)S(1)}, f32[20]{0:T(128)}, u32[]{:S(2)}) copy-start(f32[20]{0:T(128)} %slope_ref.1) | copy-start | bytes 244
  68.1 2.9 %collective-permute-start = (f32[4,168,256]{2,1,0:T(8,128)S(1)}, f32[4,168,256]{2,1,0:T(8,128)S(1)}, u32[]{:S(2)}, u32[]{:S(2)}) collective-permute-start(f32[4,168,256]{2,1,0:T(8,128)S(1)} %get-tuple-element.29), channel_id=1, source_target_pairs={{0,1},{1,0},{2,3},{3,2},{4,5},{5,4},{6,7},{7,6},{8,9},{9,8},{10,11... | collective-permute-start | bytes 2064392 | tf_op jit(solution)/shard_map/ppermute | solution.py:487

commit v6 on v5

--- a/solution.py
+++ b/solution.py
@@ -17,6 +17,7 @@
 STAT_ROWS = 5
 PAIRS = 2
 AHEAD = 3
+KEY_COLUMNS = 256
 LOG2E = math.log2(math.e)
 
 
@@ -62,6 +63,7 @@
     lengths_ref,
     slope_ref,
     core_ref,
+    index_ref,
     gathered_ref,
     k_ref,
     vt_ref,
@@ -97,7 +99,7 @@
     row = lax.broadcasted_iota(jnp.int32, (frame_count, lanes), 0)
     lane = lax.broadcasted_iota(jnp.int32, (frame_count, lanes), 1)
     invalid = [
-        jnp.where(jnp.logical_and(row >= lengths_ref[block], lane == 0), 1.0, 0.0).astype(BF16)
+        jnp.where(jnp.logical_and(row >= lengths_ref[block, index_ref[0]], lane == 0), 1.0, 0.0).astype(BF16)
         for block in range(2)
     ]
     floor_row = lax.broadcasted_iota(jnp.int32, (lanes, tokens), 0)
@@ -194,7 +196,7 @@
         theirs_ref[...] = msg_ref[1]
 
 
-def attend(lengths, slope, core, gathered, keys, values_t, dist, frame_count, columns):
+def attend(lengths, slope, core, index, gathered, keys, values_t, dist, frame_count, columns):
     near, _, tokens = gathered.shape
     rows, width = keys.shape
     head_count = slope.shape[0]
@@ -215,6 +217,7 @@
             pl.BlockSpec(memory_space=pltpu.SMEM),
             pl.BlockSpec(memory_space=pltpu.SMEM),
             pl.BlockSpec(memory_space=pltpu.SMEM),
+            pl.BlockSpec(memory_space=pltpu.SMEM),
             pl.BlockSpec(gathered.shape, lambda p: (0, 0, 0)),
             pl.BlockSpec((rows, step_rows), lambda p: (0, p)),
             pl.BlockSpec((step_rows, rows), lambda p: (p, 0)),
@@ -229,7 +232,7 @@
         ],
         compiler_params=pltpu.CompilerParams(vmem_limit_bytes=40 << 20),
         name="attend",
-    )(lengths, slope, core, gathered, keys, values_t, dist)
+    )(lengths, slope, core, index, gathered, keys, values_t, dist)
 
 
 def slab_value(values, slab, odd):
@@ -336,6 +339,10 @@
         out_ref[target] = tiles
 
 
+def project_keys_kernel(frames_ref, w_ref, out_ref):
+    out_ref[...] = jnp.dot(frames_ref[...], w_ref[...], preferred_element_type=F32).astype(BF16)
+
+
 def columns_kernel(w_ref, out_ref):
     chunks, rows, lanes = out_ref.shape
     columns, width = w_ref.shape
@@ -458,7 +465,23 @@
     queries = lax.all_to_all(queries, SEQ[1:], 0, 0)
 
     frame_rows = frames.reshape(step_count * frame_count, width)
-    keys = jnp.dot(frame_rows, w_keyval[:, :width], preferred_element_type=F32).astype(BF16)
+    keys = pl.pallas_call(
+        project_keys_kernel,
+        grid=(width // KEY_COLUMNS,),
+        in_specs=[
+            pl.BlockSpec((step_count * frame_count, width), lambda p: (0, 0)),
+            pl.BlockSpec((width, KEY_COLUMNS), lambda p: (0, p)),
+        ],
+        out_specs=pl.BlockSpec((step_count * frame_count, KEY_COLUMNS), lambda p: (0, p)),
+        out_shape=pltpu.HBM((step_count * frame_count, width), BF16),
+        compiler_params=pltpu.CompilerParams(vmem_limit_bytes=32 << 20),
+        cost_estimate=pl.CostEstimate(
+            flops=2 * step_count * frame_count * width * width,
+            transcendentals=0,
+            bytes_accessed=2 * width * (2 * step_count * frame_count + width),
+        ),
+        name="keys",
+    )(frame_rows, pltpu.with_memory_space_constraint(w_keyval, pltpu.HBM))
     late_rows = late_frames.reshape(step_count * frame_count, width)
     values_t = lax.dot_general(
         w_keyval[:, width:], late_rows, (((0,), (1,)), ((), ())), preferred_element_type=F32
@@ -469,18 +492,18 @@
     age = jnp.arange(step_count, dtype=F32)[:, None]
     dist = jnp.stack([(apart + age).reshape(tokens), apart.reshape(tokens)])
     dist = jnp.pad(dist, ((0, 6), (0, 0)))
-    own_lengths = lax.dynamic_slice(lengths, (0, own_index), (step_count, 1)).reshape(step_count)
+    index = own_index.astype(jnp.int32).reshape(1)
 
     odd = (lax.axis_index(("seq_1", "seq_2")) % 2).astype(jnp.int32).reshape(1)
     piece = 2 * width // devices
     at = (lax.axis_index("seq_0") % (across // 2)) * piece
     bound = (SLAB - at % SLAB).astype(jnp.int32).reshape(1)
     core = lax.axis_index("seq_2").astype(jnp.int32).reshape(1)
-    queries, odd, bound, core, dist, own_lengths = lax.optimization_barrier(
-        (queries, odd, bound, core, dist, own_lengths)
+    queries, odd, bound, core, dist, index = lax.optimization_barrier(
+        (queries, odd, bound, core, dist, index)
     )
     mine, theirs = attend(
-        own_lengths, head_slope, core, queries, keys, values_t, dist, frame_count, columns
+        lengths, head_slope, core, index, queries, keys, values_t, dist, frame_count, columns
     )
     theirs, asked_columns = lax.optimization_barrier((theirs, queries))
     out_columns = asked_columns[:, part:, :]

time: 130 us -> 131 us (level)
  Pallas kernels: 15.1 us -> 22.4 us
  matrix products: 15.8 us -> 9.12 us
  waiting for transfers between devices: 6.43 us -> 4.43 us
  blocking collectives: 56.9 us -> 58.7 us
    pallas_call x0 -> x1, Pallas kernels: none -> 7.69 us  [local(): pl.pallas_call(project_keys_kernel, grid=(width // KEY_COLUMNS,), in_spec...]
    dot_general x1 -> x0, matrix products: 7.69 us -> none  [local(): jnp.dot(frame_rows, w_keyval[:, :width], preferred_element_type=F32)]
    unnamed x8, local copies, waits for them, and re-layouts: 0.79 us -> 2.7 us
    all_to_all x1, blocking collectives: 19.8 us -> 21.5 us  [local(): message = lax.all_to_all(message, 'seq_0', 0, 0)]
    all_to_all x1, waiting for transfers between devices: 2.06 us -> 0.33 us  [local(): queries = lax.all_to_all(asked, 'seq_0', 0, 0)]
  transfers between devices with their start and end apart: 3 -> 3, of which waited for: 3 -> 3; matrix products, arithmetic and copies ran while one was open for 14% -> 8% of each run, Pallas kernels for 0% -> 6%
where the time goes in v6:
time: 131 us
  blocking collectives  58.7 us (45%)
  starting transfers between devices  32.4 us (25%)
  Pallas kernels  22.4 us (17%)
  matrix products  9.12 us (7%)
  waiting for transfers between devices  4.43 us (3%)
  local copies, waits for them, and re-layouts  2.73 us (2%)
    all_to_all x1, starting transfers between devices, local(): queries = lax.all_to_all(asked, 'seq_0', 0, 0)  24.5 us
    all_to_all x1, blocking collectives, local(): message = lax.all_to_all(message, 'seq_0', 0, 0)  21.5 us
    all_to_all x1, blocking collectives, spread(): return lax.all_to_all(copies, axis, 0, 0)  16.6 us
    all_to_all x1, blocking collectives, local(): partial = lax.all_to_all(partial, SEQ[1:], 0, 0)  10.7 us
    pallas_call x1, Pallas kernels, attend(): pl.pallas_call(functools.partial(attend_kernel, frame_count=frame_count,...  10.2 us
    all_to_all x1, blocking collectives, local(): message = lax.all_to_all(message, 'seq_1', 0, 0)  9.86 us
    dot_general x1, matrix products, local(): lax.dot_general(w_keyval[:, width:], late_rows, (((0,), (1,)), ((), ())),...  9.12 us
    pallas_call x1, Pallas kernels, local(): pl.pallas_call(project_keys_kernel, grid=(width // KEY_COLUMNS,), in_spec...  7.69 us
  transfers between devices with their start and end apart: 3, of which 3 were waited for; matrix products, arithmetic and copies ran while one was open for 8% of the time, Pallas kernels for 6%

profile of v6, /device:TPU:33, one launch (start us, length us, event | category | flops | bytes accessed | tf_op | source)
XLA Modules:
  0.0 130.6 jit_solution(16164437889451779131)
XLA Ops:
  0.0 2.1 %ask.1 = bf16[16,4,640]{2,1,0:T(4,128)(2,1)} custom-call(bf16[10,1280]{1,0:T(8,128)(2,1)} %bitcast.19, bf16[256,1280]{1,0:T(8,128)(2,1)} %bitcast.18), custom_call_target="tpu_custom_call" | custom-call | tf_op jit(solution)/shard_map/ask/pallas_call | solution.py:407
  2.1 24.5 %all-to-all-start = ((bf16[16,4,640]{2,1,0:T(4,128)(2,1)}), bf16[16,4,640]{2,1,0:T(4,128)(2,1)S(1)}, u32[]{:S(2)}, u32[]{:S(2)}) async-start(bf16[16,4,640]{2,1,0:T(4,128)(2,1)} %ask.1), calls=%async_computation | async-start | bytes 163840 | tf_op jit(solution)/shard_map/all_to_all | solution.py:455
  26.7 0.0 copy-start
  26.7 0.8 copy-done
  27.4 0.1 columns.1.w_ref
  27.5 0.7 iota_add_fusion
  28.2 0.0 copy-start.3
  28.2 1.9 %copy-done.3 = bf16[2,640,1280]{2,1,0:T(8,128)(2,1)S(1)} copy-done((bf16[2,640,1280]{2,1,0:T(8,128)(2,1)S(1)}, bf16[2,640,1280]{2,1,0:T(8,128)(2,1)}, u32[]{:S(2)}) %copy-start.3) | copy-done | bytes 3276824
  30.2 7.7 %keys.1.k_ref = bf16[1280,1280]{1,0:T(8,128)(2,1)} custom-call(bf16[1280,1280]{1,0:T(8,128)(2,1)S(1)} %bitcast.17, bf16[1280,2560]{1,0:T(8,128)(2,1)} %w_ref.1), custom_call_target="tpu_custom_call" | custom-call | flops 4194304000 | bytes 9830400 | tf_op jit(solution)/shard_map/keys/pallas_call | solution.py:468
  37.9 0.3 all-to-all-done.tiles_ref
  38.2 1.0 pack.1
  39.1 6.8 %all-to-all-start.1 = ((bf16[8,176,256]{2,1,0:T(8,128)(2,1)}), bf16[8,176,256]{2,1,0:T(8,128)(2,1)S(1)}, u32[]{:S(2)}, u32[]{:S(2)}) async-start(bf16[8,176,256]{2,1,0:T(8,128)(2,1)} %pack.1), calls=%async_computation.1 | async-start | bytes 1441792 | tf_op jit(solution)/shard_map/all_to_all | solution.py:465
  46.0 0.0 copy-start.1
  46.0 0.0 copy-start.2
  46.0 9.1 %fusion.vt_ref = bf16[1280,1280]{1,0:T(8,128)(2,1)} fusion(bf16[1280,1280]{1,0:T(8,128)(2,1)} %bitcast.16, bf16[1280,2560]{1,0:T(8,128)(2,1)} %w_ref.1), kind=kOutput, calls=%fused_computation.1 | convolution fusion | flops 4195942400 | bytes 9830400 | tf_op jit(solution)/shard_map/dot_general | solution.py:486
  55.1 2.3 %all-to-all-done.1.gathered_ref = bf16[8,176,256]{2,1,0:T(8,128)(2,1)S(1)} async-done(((bf16[8,176,256]{2,1,0:T(8,128)(2,1)}), bf16[8,176,256]{2,1,0:T(8,128)(2,1)S(1)}, u32[]{:S(2)}, u32[]{:S(2)}) %all-to-all-start.1) | async-done | bytes 720928 | tf_op jit(solution)/shard_map/all_to_all | solution.py:465
  57.4 0.0 copy-done.1
  57.4 0.0 copy-done.2
  57.4 10.2 %attend.1 = (f32[4,168,256]{2,1,0:T(8,128)S(1)}, f32[4,168,256]{2,1,0:T(8,128)S(1)}) custom-call(s32[2,128]{1,0:T(2,128)S(1)} %copy-done.1, f32[20]{0:T(128)S(1)} %copy-done.2, s32[1]{0:T(128)} %bitcast.5.core_ref, s32[1]{0:T(128)} %bitcast.8.index_ref, bf16[8,176,256]{2,1,0:T(8,128)(2,1)S(1)} %all-to-all-done.1.gathered_ref, bf16[1280,1280]{1,0:T(8,128)(2,1)} %keys.1.k_ref, ...), custom_call_target="tpu_custom_call" | custom-call | tf_op jit(solution)/shard_map/attend/pallas_call | solution.py:207
  67.7 1.1 collective-permute-start
  68.8 1.8 %collective-permute-done.theirs_ref = f32[4,168,256]{2,1,0:T(8,128)S(1)} collective-permute-done((f32[4,168,256]{2,1,0:T(8,128)S(1)}, f32[4,168,256]{2,1,0:T(8,128)S(1)}, u32[]{:S(2)}, u32[]{:S(2)}) %collective-permute-start) | collective-permute-done | bytes 688160 | tf_op jit(solution)/shard_map/ppermute | solution.py:510
  70.5 0.2 join.1
  70.7 9.9 %all_to_all.30.in_ref = bf16[4,176,256]{2,1,0:T(8,128)(2,1)S(1)} all-to-all(bf16[4,176,256]{2,1,0:T(8,128)(2,1)S(1)} %join.1), channel_id=1, replica_groups=mesh['grp'=2,'seq_0'=16,'seq_1'=4,'seq_2'=2] {'seq_1'}, dimensions={0} | all-to-all | bytes 720896 | tf_op jit(solution)/shard_map/all_to_all | solution.py:519
  80.6 0.2 merge.1
  80.8 21.5 %all_to_all.31.in_ref = bf16[16,4,896]{2,1,0:T(4,128)(2,1)S(1)} all-to-all(bf16[16,4,896]{2,1,0:T(4,128)(2,1)S(1)} %merge.1), channel_id=1, replica_groups=mesh['grp'=2,'seq_0'=16,'seq_1'=4,'seq_2'=2] {'seq_0'}, dimensions={0} | all-to-all | bytes 229376 | tf_op jit(solution)/shard_map/all_to_all | solution.py:527
  102.3 0.1 finish.1
  102.5 16.6 %all_to_all.32.ctx_ref = bf16[16,4,640]{2,1,0:T(4,128)(2,1)S(1)} all-to-all(bf16[16,4,640]{2,1,0:T(4,128)(2,1)S(1)} %broadcast_in_dim.2), channel_id=1, replica_groups=mesh['grp'=2,'seq_0'=16,'seq_1'=4,'seq_2'=2] {'seq_0'}, dimensions={0} | all-to-all | bytes 163840 | tf_op jit(solution)/shard_map/all_to_all | solution.py:422
  119.1 0.2 project.1
  119.2 10.7 %all_to_all.33.in_ref = f32[8,16,256]{2,1,0:T(8,128)S(1)} all-to-all(f32[8,16,256]{2,1,0:T(8,128)S(1)} %project.1), channel_id=1, replica_groups=mesh['grp'=2,'seq_0'=16,'seq_1'=4,'seq_2'=2] {'seq_1','seq_2'}, dimensions={0} | all-to-all | bytes 262144 | tf_op jit(solution)/shard_map/all_to_all | solution.py:544
  130.0 0.6 sum.1
  (3 shorter events, 0.0 us)
Async XLA Ops:
  2.1 36.1 %all-to-all-start = ((bf16[16,4,640]{2,1,0:T(4,128)(2,1)}), bf16[16,4,640]{2,1,0:T(4,128)(2,1)S(1)}, u32[]{:S(2)}, u32[]{:S(2)}) async-start(bf16[16,4,640]{2,1,0:T(4,128)(2,1)} %ask.1), calls=%async_computation | async-start | bytes 163840 | tf_op jit(solution)/shard_map/all_to_all | solution.py:455
  26.7 0.8 copy-start
  28.2 1.9 %copy-start.3 = (bf16[2,640,1280]{2,1,0:T(8,128)(2,1)S(1)}, bf16[2,640,1280]{2,1,0:T(8,128)(2,1)}, u32[]{:S(2)}) copy-start(bf16[2,640,1280]{2,1,0:T(8,128)(2,1)} %param.8) | copy-start | bytes 9830404
  39.1 18.3 %all-to-all-start.1 = ((bf16[8,176,256]{2,1,0:T(8,128)(2,1)}), bf16[8,176,256]{2,1,0:T(8,128)(2,1)S(1)}, u32[]{:S(2)}, u32[]{:S(2)}) async-start(bf16[8,176,256]{2,1,0:T(8,128)(2,1)} %pack.1), calls=%async_computation.1 | async-start | bytes 1441792 | tf_op jit(solution)/shard_map/all_to_all | solution.py:465
  46.0 11.5 %copy-start.1 = (s32[2,128]{1,0:T(2,128)S(1)}, s32[2,128]{1,0:T(2,128)}, u32[]{:S(2)}) copy-start(s32[2,128]{1,0:T(2,128)} %lengths_ref.1) | copy-start | bytes 3076
  46.0 11.5 %copy-start.2 = (f32[20]{0:T(128)S(1)}, f32[20]{0:T(128)}, u32[]{:S(2)}) copy-start(f32[20]{0:T(128)} %slope_ref.1) | copy-start | bytes 244
  67.7 2.9 %collective-permute-start = (f32[4,168,256]{2,1,0:T(8,128)S(1)}, f32[4,168,256]{2,1,0:T(8,128)S(1)}, u32[]{:S(2)}, u32[]{:S(2)}) collective-permute-start(f32[4,168,256]{2,1,0:T(8,128)S(1)} %get-tuple-element.29), channel_id=1, source_target_pairs={{0,1},{1,0},{2,3},{3,2},{4,5},{5,4},{6,7},{7,6},{8,9},{9,8},{10,11... | collective-permute-start | bytes 2064392 | tf_op jit(solution)/shard_map/ppermute | solution.py:510
